TPU v7x, 32 devices: a whole 2x2x4 slice. The times are simulated.
32 devices in a mesh: dp: 8 (over z, core), mp: 4 (over y, x).
Axes of the slice: x: 2, y: 2, z: 4, core: 2. Of those that a mesh axis runs over, the one named last changes fastest.
Arguments:
- master: float32 [4096, 5120], P('dp', 'mp'), may hold values from -60 to 60
- moment_first: float32 [4096, 5120], P('dp', 'mp'), may hold values from -0.06 to 0.06
- moment_second: float32 [4096, 5120], P('dp', 'mp'), may hold values from 1e-05 to 0.001
- gradients: float32 [4096, 5120], P('dp', 'mp'), may hold values from -0.2 to 0.2
- step_count: int32 [1], replicated, may hold values from 1 to 10
- tensor_rows: int32 [24], replicated, may hold values from 1 to 1024, 4096 in all
- decay_mask: int32 [24], replicated, may hold values 0 or 1
Outputs:
- new_master: float32 [4096, 5120], P('dp', 'mp')
- new_first: float32 [4096, 5120], P('dp', 'mp')
- new_second: float32 [4096, 5120], P('dp', 'mp')
- compute_weights: bfloat16 [4096, 5120], P(None, 'mp')
Inputs may be any that keep to these rules, and one draw needn't show every extreme that they name: `tensor_rows`: the rows sum to 4096; the largest tensor has 1024 rows.
All inputs are finite; a program needn't handle non-finite values.
Results may differ from a plain program's by a relative error of at most 0.0004.
Values may be sent and summed in bfloat16 or wider, within the bound.
No kernel may reach another device: no remote copies, remote signals or barrier semaphores. Data moves between devices by JAX's collectives and lax.ppermute only.
A program may use at most 128 MiB of HBM per device.

v0:
```python
import jax
import jax.numpy as jnp
from jax import lax
from jax.sharding import PartitionSpec as P

beta_first = 0.9
beta_second = 0.999
adam_epsilon = 1e-06
decay_rate = 0.3
learn_rate = 0.3
norm_epsilon = 1e-06


def membership(first_row, count, offsets, tensor_rows):
    row_ids = first_row + jnp.arange(count, dtype=jnp.int32)
    inside = (row_ids[None, :] >= offsets[:, None]) & (
        row_ids[None, :] < (offsets + tensor_rows)[:, None]
    )
    return inside.astype(jnp.float32)


def local(master, moment_first, moment_second, gradients, step_count, tensor_rows, decay_mask):
    rows_dev = master.shape[0]
    steps = step_count[0].astype(jnp.float32)
    new_first = beta_first * moment_first + (1.0 - beta_first) * gradients
    new_second = beta_second * moment_second + (1.0 - beta_second) * gradients * gradients
    fix_first = 1.0 - jnp.power(jnp.float32(beta_first), steps)
    fix_second = 1.0 - jnp.power(jnp.float32(beta_second), steps)
    offsets = jnp.cumsum(tensor_rows) - tensor_rows
    first_row = lax.axis_index("dp") * rows_dev
    member = membership(first_row, rows_dev, offsets, tensor_rows)
    mask_rows = jnp.dot(decay_mask.astype(jnp.float32), member, precision=lax.Precision.HIGHEST)
    update = new_first / fix_first / (jnp.sqrt(new_second / fix_second) + adam_epsilon)
    update = update + decay_rate * mask_rows[:, None] * master
    weight_part = jnp.dot(member, jnp.sum(master * master, axis=1), precision=lax.Precision.HIGHEST)
    update_part = jnp.dot(member, jnp.sum(update * update, axis=1), precision=lax.Precision.HIGHEST)
    column_sums = lax.psum((weight_part, update_part), "mp")
    weight_sq, update_sq = lax.psum((column_sums[0], column_sums[1]), "dp")
    ratio = jnp.sqrt(weight_sq) / (jnp.sqrt(update_sq) + norm_epsilon)
    ratio_rows = jnp.dot(ratio, member, precision=lax.Precision.HIGHEST)
    new_master = master - learn_rate * ratio_rows[:, None] * update
    compute_weights = lax.all_gather(new_master.astype(jnp.bfloat16), "dp", axis=0, tiled=True)
    return (new_master, new_first, new_second, compute_weights)


def solution(mesh):
    placed = (P("dp", "mp"), P("dp", "mp"), P("dp", "mp"), P("dp", "mp"), P(), P(), P())
    return jax.shard_map(
        local,
        mesh=mesh,
        in_specs=placed,
        out_specs=(P("dp", "mp"), P("dp", "mp"), P("dp", "mp"), P(None, "mp")),
        check_vma=False,
    )
```

profile of v0, /device:TPU:0, one launch (start us, length us, event | category | flops | bytes accessed | tf_op | source)
XLA Modules:
  0.0 159.5 jit_solution(13009378844300602519)
XLA Ops:
  7.2 0.0 all-gather.2.cloned.1.call-start
  8.0 0.7 copy.12
  8.7 0.1 reduce
  8.9 0.7 sub.18
  9.5 0.1 compare_and_fusion
  9.6 0.8 fusion.2
  10.4 0.0 copy-start
  10.4 7.1 %multiply_reduce_fusion = (f32[512]{0:T(512)S(1)}, f32[512,1280]{1,0:T(8,128)}, f32[512,1280]{1,0:T(8,128)}, f32[512,1280]{1,0:T(8,128)}, f32[512]{0:T(512)S(1)}) fusion(f32[512,1280]{1,0:T(8,128)} %param.7, f32[512]{0:T(512)S(1)} %broadcast_multiply_fusion.1, f32[]{:T(128)} %bitcast.4, f32[]{:T(128)} %bitcast.3, f32[512,1280]{1,0:T(8,128)} %param.10, ...), kind=kLoop, calls=%fused_computation.3 | loop fusion | flops 11140096 | bytes 18356232 | tf_op jit(solution)/shard_map/reduce_sum | solution.py:36
  17.5 0.1 convolution_bitcast_fusion
  17.6 0.1 convolution_bitcast_fusion.1
  17.7 11.4 %all-reduce.1 = (f32[24]{0:T(128)S(1)}, f32[24]{0:T(128)S(1)}) all-reduce(f32[24]{0:T(128)S(1)} %convolution_bitcast_fusion, f32[24]{0:T(128)S(1)} %convolution_bitcast_fusion.1), channel_id=1, replica_groups=mesh['dp'=8,'mp'=4] {'mp'}, use_global_device_ids=true, to_apply=%region_5.6 | all-reduce | flops 48 | bytes 384 | tf_op jit(solution)/shard_map/psum | solution.py:37
  29.1 14.6 %all-reduce = (f32[24]{0:T(128)S(1)}, f32[24]{0:T(128)S(1)}) all-reduce(f32[24]{0:T(128)S(1)} %get-tuple-element.6, f32[24]{0:T(128)S(1)} %get-tuple-element.7), channel_id=1, replica_groups=mesh['dp'=8,'mp'=4] {'dp'}, use_global_device_ids=true, to_apply=%region_6.7 | all-reduce | flops 48 | bytes 384 | tf_op jit(solution)/shard_map/psum | solution.py:38
  43.7 0.1 fusion.3
  43.9 0.0 copy-done
  43.9 4.0 %fusion.7 = (bf16[512,1280]{1,0:T(8,128)(2,1)}, f32[512,1280]{1,0:T(8,128)}) fusion(f32[512,1280]{1,0:T(8,128)S(1)} %copy-done, f32[512,1280]{1,0:T(8,128)} %get-tuple-element.11, f32[512]{0:T(512)S(1)} %broadcast_multiply_fusion), kind=kLoop, calls=%fused_computation.20 | loop fusion | flops 1966080 | bytes 9177088 | tf_op jit(solution)/shard_map/convert_element_type | solution.py:42
  47.9 0.0 all-gather.2.cloned.1.call-update
  47.9 96.0 %all-gather.2.cloned.1.call-done = bf16[4096,1280]{1,0:T(8,128)(2,1)} async-done(((bf16[512,1280]{1,0:T(8,128)(2,1)}), bf16[4096,1280]{1,0:T(8,128)(2,1)}) %all-gather.2.cloned.1.call-update) | async-done | bytes 10485776 | tf_op jit(solution)/shard_map/all_gather | solution.py:42
  144.0 8.7 %copy.15 = bf16[4096,1280]{1,0:T(8,128)(2,1)} copy(bf16[4096,1280]{1,0:T(8,128)(2,1)} %all-gather.2.cloned.1.call-done) | data formatting | bytes 20971520
  (4 shorter events, 0.1 us)
Async XLA Ops:
  7.2 136.8 %all-gather.2.cloned.1.call-start = ((), (), s32[]{:S(2)}) async-start(), calls=%async_computation | async-start | bytes 11796480 | tf_op jit(solution)/shard_map/all_gather | solution.py:42
  10.4 33.5 %copy-start = (f32[512,1280]{1,0:T(8,128)S(1)}, f32[512,1280]{1,0:T(8,128)}, u32[]{:S(2)}) copy-start(f32[512,1280]{1,0:T(8,128)} %param.7) | copy-start | bytes 7864324
Sparse Core Ops, SparseCore 0:
  48.1 95.8 all-gather.1
where the time goes:
time: 160 us
  waiting for transfers between devices  96 us (60%)
  blocking collectives  26 us (16%)
  between operations  14.8 us (9%)
  other arithmetic  12 us (8%)
  local copies, waits for them, and re-layouts  9.48 us (6%)
    all_gather x1, waiting for transfers between devices, local(): lax.all_gather(new_master.astype(jnp.bfloat16), 'dp', axis=0, tiled=True)  96 us
    psum x1, blocking collectives, local(): weight_sq, update_sq = lax.psum((column_sums[0], column_sums[1]), 'dp')  14.6 us
    psum x1, blocking collectives, local(): column_sums = lax.psum((weight_part, update_part), 'mp')  11.4 us
    unnamed x3, local copies, waits for them, and re-layouts  8.74 us
    reduce_sum x1, other arithmetic, local(): jnp.sum(update * update, axis=1)  7.08 us
    convert_element_type x1, other arithmetic, local(): new_master.astype(jnp.bfloat16)  4.02 us
  transfers between devices with their start and end apart: 1, of which 1 were waited for; matrix products, arithmetic and copies ran while one was open for 0% of the time, Pallas kernels for 0%

commit v1 on v0

v1 whole, which is shorter than its diff:
```python
import functools

import jax
import jax.numpy as jnp
from jax import lax
from jax.experimental import pallas as pl
from jax.experimental.pallas import tpu as pltpu
from jax.sharding import PartitionSpec as P


beta_first = 0.9
beta_second = 0.999
adam_epsilon = 1e-06
decay_rate = 0.3
learn_rate = 0.3
norm_epsilon = 1e-06

LANES = 128
PIECES = 8
CHUNKS = 2
MIB = 1024 * 1024
f32, bf16 = jnp.float32, jnp.bfloat16
hbm = pl.BlockSpec(memory_space=pltpu.HBM)
vmem = pl.BlockSpec(memory_space=pltpu.VMEM)


def in_hbm(*arrays):
    return tuple(pltpu.with_memory_space_constraint(a, pltpu.HBM) for a in arrays)


def power(base, steps):
    return lax.fori_loop(0, steps, lambda _, p: p * base, jnp.float32(1.0))


def first_pass(step_count, rows_hbm, decay_hbm, master, moment_first, moment_second, gradients,
               kept_master, kept_first, kept_second, kept_update, member, sums,
               weight_rows, update_rows, mask_rows, tensor_rows, decay_mask, small_sems, sems):
    rows, cols = kept_master.shape
    piece = rows // PIECES
    small = []
    for a, (source, target) in enumerate(((rows_hbm, tensor_rows), (decay_hbm, decay_mask))):
        copy = pltpu.make_async_copy(source, target, small_sems.at[a])
        copy.start()
        small.append(copy)
    copies = []
    for p in range(PIECES):
        part = pl.ds(p * piece, piece)
        for a, (source, target) in enumerate((
            (master, kept_master), (moment_first, kept_first), (moment_second, kept_second), (gradients, kept_update),
        )):
            copy = pltpu.make_async_copy(source.at[part], target.at[part], sems.at[a, p])
            copy.start()
            copies.append(copy)
    for copy in small:
        copy.wait()

    steps = step_count[0]
    scale_first = 1.0 / (1.0 - jnp.full((8, LANES), power(jnp.float32(beta_first), steps)))
    scale_second = 1.0 / (1.0 - jnp.full((8, LANES), power(jnp.float32(beta_second), steps)))
    lane = lax.broadcasted_iota(jnp.int32, (8, LANES), 1)
    start = jnp.zeros((8, LANES), jnp.int32)
    end = jnp.zeros((8, LANES), jnp.int32)
    decay = jnp.zeros((8, LANES), f32)
    offset = jnp.int32(0)
    for k in range(tensor_rows.shape[0]):
        after = offset + tensor_rows[k]
        start = jnp.where(lane == k, offset, start)
        end = jnp.where(lane == k, after, end)
        decay = jnp.where(lane == k, decay_rate * decay_mask[k].astype(f32), decay)
        offset = after
    row = lax.axis_index("dp") * rows + lax.broadcasted_iota(jnp.int32, (8, LANES), 0)

    def belongs(i, carry):
        at = pl.ds(pl.multiple_of(i * 8, 8), 8)
        here = row + i * 8
        inside = jnp.where((here >= start) & (here < end), 1.0, 0.0)
        member[at] = inside
        mask_rows[at] = jnp.broadcast_to(jnp.sum(inside * decay, axis=1, keepdims=True), (8, LANES))
        return carry

    lax.fori_loop(0, rows // 8, belongs, 0, unroll=4)

    for p in range(PIECES):
        for copy in copies[4 * p:4 * p + 4]:
            copy.wait()

        def group(i, carry):
            at = pl.ds(pl.multiple_of(p * piece + i * 8, 8), 8)
            mask = mask_rows[at]
            weight = jnp.zeros((8, LANES), f32)
            total = jnp.zeros((8, LANES), f32)
            for t in range(cols // LANES):
                tile = (at, pl.ds(t * LANES, LANES))
                grad = kept_update[tile]
                value = kept_master[tile]
                new_first = beta_first * kept_first[tile] + (1.0 - beta_first) * grad
                new_second = beta_second * kept_second[tile] + (1.0 - beta_second) * grad * grad
                update = (new_first * scale_first) / (jnp.sqrt(new_second * scale_second) + adam_epsilon)
                update = update + mask * value
                kept_first[tile] = new_first
                kept_second[tile] = new_second
                kept_update[tile] = update
                weight = weight + value * value
                total = total + update * update
            weight_rows[at] = weight
            update_rows[at] = total
            return carry

        lax.fori_loop(0, piece // 8, group, 0)

    dims = (((0,), (0,)), ((), ()))
    dot = functools.partial(lax.dot_general, dimension_numbers=dims, precision=lax.Precision.HIGHEST, preferred_element_type=f32)
    per_weight = jnp.sum(dot(weight_rows[...], member[...]), axis=0, keepdims=True)
    per_update = jnp.sum(dot(update_rows[...], member[...]), axis=0, keepdims=True)
    both = jnp.concatenate([per_weight, per_update], axis=0)
    sums[...] = jnp.broadcast_to(both[None], sums.shape)


def rate_rows(sums, member):
    total = jnp.sum(sums[...], axis=0)
    ratio = jnp.sqrt(total[0:1]) / (jnp.sqrt(total[1:2]) + norm_epsilon)
    return jnp.sum(member * (learn_rate * ratio), axis=1, keepdims=True)


def round_pass(first, sums, member, kept_master, kept_update, chunk):
    part = pl.ds(first, chunk.shape[0])
    rate = rate_rows(sums, member[part])
    chunk[...] = (kept_master[part] - rate * kept_update[part]).astype(bf16)


def write_pass(sums, member, kept_master, kept_first, kept_second, kept_update,
               new_master, new_first, new_second, gathered, wide, narrow, sems):
    rows = kept_master.shape[0]
    one = pltpu.make_async_copy(kept_first, new_first, sems.at[0])
    two = pltpu.make_async_copy(kept_second, new_second, sems.at[1])
    one.start()
    two.start()
    wide[...] = kept_master[...] - rate_rows(sums, member[...]) * kept_update[...]
    narrow[...] = wide[...].astype(bf16)
    mine = pl.ds(pl.multiple_of(lax.axis_index("dp") * rows, rows), rows)
    three = pltpu.make_async_copy(wide, new_master, sems.at[2])
    four = pltpu.make_async_copy(narrow, gathered.at[mine], sems.at[3])
    three.start()
    four.start()
    for copy in (one, two, three, four):
        copy.wait()


def place_pass(chips, rows, items, before, *refs):
    pieces, (gathered, sems) = refs[:len(items)], refs[len(items):]
    me = lax.axis_index("dp")
    chip, core = me // 2, me % 2
    spot = jnp.where(chip % 2 == 0, chip // 2, chips - (chip + 1) // 2)
    copies = []
    for a, (step, swapped, first) in enumerate(items):
        at = (spot + chips - step) % chips
        source = jnp.where(2 * at < chips, 2 * at, 2 * (chips - at) - 1)
        owner = 2 * source + (1 - core if swapped else core)
        part = pl.ds(pl.multiple_of(owner * rows + first, 16), pieces[a].shape[0])
        copies.append(pltpu.make_async_copy(pieces[a], gathered.at[part], sems.at[a]))
        copies[-1].start()
    for copy in copies:
        copy.wait()


def place(chips, rows, items, gathered, *pieces):
    return pl.pallas_call(
        functools.partial(place_pass, chips, rows, items),
        out_shape=pltpu.HBM(gathered.shape, gathered.dtype),
        in_specs=[hbm] + [vmem] * len(items),
        out_specs=hbm,
        scratch_shapes=[pltpu.SemaphoreType.DMA((len(items),))],
        input_output_aliases={0: 0},
        compiler_params=pltpu.CompilerParams(vmem_limit_bytes=4 * MIB),
        name="place_pass",
    )(*in_hbm(gathered), *pieces)


def local(devices, dp, master, moment_first, moment_second, gradients, step_count, tensor_rows, decay_mask):
    rows, cols = master.shape
    kept = pltpu.VMEM((rows, cols), f32)
    small = [pltpu.SMEM(a.shape, a.dtype) for a in (tensor_rows, decay_mask)]

    kept_master, kept_first, kept_second, kept_update, member, sums = pl.pallas_call(
        first_pass,
        out_shape=(kept, kept, kept, kept, pltpu.VMEM((rows, LANES), f32), jax.ShapeDtypeStruct((devices, 2, LANES), f32)),
        in_specs=[pl.BlockSpec(memory_space=pltpu.SMEM)] + [hbm] * 6,
        out_specs=(vmem,) * 6,
        scratch_shapes=[pltpu.VMEM((rows, LANES), f32)] * 3 + small
        + [pltpu.SemaphoreType.DMA((2,)), pltpu.SemaphoreType.DMA((4, PIECES))],
        compiler_params=pltpu.CompilerParams(vmem_limit_bytes=4 * MIB),
        name="first_pass",
    )(step_count, *in_hbm(tensor_rows, decay_mask, master, moment_first, moment_second, gradients))

    sums = lax.all_to_all(sums, ("dp", "mp"), 0, 0, tiled=True)

    size = rows // CHUNKS
    pieces = []
    for i in range(CHUNKS):
        pieces.append(pl.pallas_call(
            functools.partial(round_pass, i * size),
            out_shape=pltpu.VMEM((size, cols), bf16),
            in_specs=[vmem] * 4,
            out_specs=vmem,
            compiler_params=pltpu.CompilerParams(vmem_limit_bytes=4 * MIB),
            name="round_pass",
        )(sums, member, kept_master, kept_update))

    new_master, new_first, new_second, gathered = pl.pallas_call(
        write_pass,
        out_shape=(jax.ShapeDtypeStruct((rows, cols), f32),) * 3 + (pltpu.HBM((dp * rows, cols), bf16),),
        in_specs=[vmem] * 6,
        out_specs=(hbm,) * 4,
        scratch_shapes=[pltpu.VMEM((rows, cols), f32), pltpu.VMEM((rows, cols), bf16), pltpu.SemaphoreType.DMA((4,))],
        compiler_params=pltpu.CompilerParams(vmem_limit_bytes=8 * MIB),
        name="write_pass",
    )(sums, member, kept_master, kept_first, kept_second, kept_update)

    chips = dp // 2
    order = [2 * p if 2 * p < chips else 2 * (chips - p) - 1 for p in range(chips)]
    ring = [(2 * order[p] + c, 2 * order[(p + 1) % chips] + c) for p in range(chips) for c in range(2)]
    partner = [(d, d ^ 1) for d in range(dp)]
    others = []
    for k in range(chips):
        for i in range(CHUNKS):
            piece, first = pieces[i], i * size
            if k < chips - 1:
                pieces[i] = lax.ppermute(piece, "dp", ring)
            other = lax.ppermute(piece, "dp", partner)
            if k == 0:
                others.append(other)
                if i == CHUNKS - 1:
                    gathered = place(chips, rows, tuple((0, True, j * size) for j in range(CHUNKS)), gathered, *others)
            elif k == chips - 1 and i == CHUNKS - 1:
                gathered = place(chips, rows, ((k, False, first),), gathered, piece)
                gathered = place(chips, rows, ((k, True, first),), gathered, other)
            else:
                gathered = place(chips, rows, ((k, False, first), (k, True, first)), gathered, piece, other)
    return new_master, new_first, new_second, gathered


def solution(mesh):
    placed = (P("dp", "mp"), P("dp", "mp"), P("dp", "mp"), P("dp", "mp"), P(), P(), P())
    body = functools.partial(local, mesh.size, mesh.shape["dp"])

    return jax.shard_map(
        body,
        mesh=mesh,
        in_specs=placed,
        out_specs=(P("dp", "mp"), P("dp", "mp"), P("dp", "mp"), P(None, "mp")),
        check_vma=False,
    )
```

time: 160 us -> 121 us (0.76)
  Pallas kernels: 0 us -> 18.7 us
  waiting for transfers between devices: 96 us -> 77.9 us
  between operations: 14.8 us -> 1.42 us
  other arithmetic: 12 us -> 0 us
  blocking collectives: 26 us -> 14.4 us
  local copies, waits for them, and re-layouts: 9.48 us -> 0 us
  starting transfers between devices: 0.04 us -> 8.43 us
    all_gather x1 -> x0, waiting for transfers between devices: 96 us -> none  [local(): lax.all_gather(new_master.astype(jnp.bfloat16), 'dp', axis=0, tiled=True)]
    ppermute x0 -> x14, waiting for transfers between devices: none -> 77.9 us  [the longest x6 77.9 us: local(): pieces[i] = lax.ppermute(piece, 'dp', ring)]
    psum x2 -> x0, blocking collectives: 26 us -> none  [the longest x1 14.6 us: local(): weight_sq, update_sq = lax.psum((column_sums[0], column_sums[1]), 'dp')]
    pallas_call x0 -> x12, Pallas kernels: none -> 18.7 us  [the longest x8 8.43 us: place(): pl.pallas_call(functools.partial(place_pass, chips, rows, items), out_sha...]
    all_to_all x0 -> x1, blocking collectives: none -> 14.4 us  [local(): sums = lax.all_to_all(sums, ('dp', 'mp'), 0, 0, tiled=True)]
    unnamed x3 -> x0, local copies, waits for them, and re-layouts: 8.74 us -> none
    ppermute x0 -> x14, starting transfers between devices: none -> 8.43 us  [the longest x6 7.34 us: local(): pieces[i] = lax.ppermute(piece, 'dp', ring)]
    reduce_sum x1 -> x0, other arithmetic: 7.08 us -> none  [local(): jnp.sum(update * update, axis=1)]
  transfers between devices with their start and end apart: 1 -> 14, of which waited for: 1 -> 6; matrix products, arithmetic and copies ran while one was open for 0% -> 0% of each run, Pallas kernels for 0% -> 9%
where the time goes in v1:
time: 121 us
  waiting for transfers between devices  77.9 us (64%)
  Pallas kernels  18.7 us (15%)
  blocking collectives  14.4 us (12%)
  starting transfers between devices  8.43 us (7%)
  between operations  1.42 us (1%)
    ppermute x6, waiting for transfers between devices, local(): pieces[i] = lax.ppermute(piece, 'dp', ring)  77.9 us
    all_to_all x1, blocking collectives, local(): sums = lax.all_to_all(sums, ('dp', 'mp'), 0, 0, tiled=True)  14.4 us
    pallas_call x8, Pallas kernels, place(): pl.pallas_call(functools.partial(place_pass, chips, rows, items), out_sha...  8.43 us
    ppermute x6, starting transfers between devices, local(): pieces[i] = lax.ppermute(piece, 'dp', ring)  7.34 us
    pallas_call x1, Pallas kernels, local(): pl.pallas_call(first_pass, out_shape=(kept, kept, kept, kept, pltpu.VMEM(...  6.2 us
    pallas_call x1, Pallas kernels, local(): pl.pallas_call(write_pass, out_shape=(jax.ShapeDtypeStruct((rows, cols),...  3.61 us
  transfers between devices with their start and end apart: 14, of which 6 were waited for; matrix products, arithmetic and copies ran while one was open for 0% of the time, Pallas kernels for 9%

profile of v1, /device:TPU:0, one launch (start us, length us, event | category | flops | bytes accessed | tf_op | source)
XLA Modules:
  0.0 120.9 jit_solution(16285043833640047343)
XLA Ops:
  1.3 6.2 %first_pass.1 = (f32[512,1280]{1,0:T(8,128)S(1)}, f32[512,1280]{1,0:T(8,128)S(1)}, f32[512,1280]{1,0:T(8,128)S(1)}, f32[512,1280]{1,0:T(8,128)S(1)}, f32[512,128]{1,0:T(8,128)S(1)}, /*index=5*/f32[32,2,128]{2,1,0:T(2,128)S(1)}) custom-call(s32[1]{0:T(128)S(6)} %copy.27.step_count, s32[24]{0:T(128)} %rows_hbm.1, s32[24]{0:T(128)} %decay_hbm.1, ...), custom_call_target="tpu_custom_call" | custom-call | tf_op jit(solution)/shard_map/first_pass/pallas_call | solution.py:184
  7.5 14.4 %all_to_all.5.sums = f32[32,2,128]{2,1,0:T(2,128)S(1)} all-to-all(f32[32,2,128]{2,1,0:T(2,128)S(1)} %get-tuple-element.14), channel_id=1, replica_groups=mesh['dp'=8,'mp'=4] {'dp','mp'}, dimensions={0} | all-to-all | bytes 65536 | tf_op jit(solution)/shard_map/all_to_all | solution.py:195
  22.2 0.7 collective-permute-start.2
  23.1 0.6 collective-permute-start.4
  23.7 16.1 %collective-permute-done.2.refs_0_ = bf16[256,1280]{1,0:T(8,128)(2,1)S(1)} collective-permute-done((bf16[256,1280]{1,0:T(8,128)(2,1)S(1)}, bf16[256,1280]{1,0:T(8,128)(2,1)S(1)}, u32[]{:S(2)}, u32[]{:S(2)}) %collective-permute-start.2) | collective-permute-done | bytes 655392 | tf_op jit(solution)/shard_map/ppermute | solution.py:228
  39.8 1.5 %collective-permute-start.6 = (bf16[256,1280]{1,0:T(8,128)(2,1)S(1)}, bf16[256,1280]{1,0:T(8,128)(2,1)S(1)}, u32[]{:S(2)}, u32[]{:S(2)}) collective-permute-start(bf16[256,1280]{1,0:T(8,128)(2,1)S(1)} %collective-permute-done.2.refs_0_), channel_id=1, source_target_pairs={{0,16},{4,20},{16,24},{20,28},{24,8},{28,12},{8,0},{12,4},{1,17},{... | collective-permute-start | bytes 1966088 | tf_op jit(solution)/shard_map/ppermute | solution.py:228
  41.3 12.5 %collective-permute-done.4.refs_0_ = bf16[256,1280]{1,0:T(8,128)(2,1)S(1)} collective-permute-done((bf16[256,1280]{1,0:T(8,128)(2,1)S(1)}, bf16[256,1280]{1,0:T(8,128)(2,1)S(1)}, u32[]{:S(2)}, u32[]{:S(2)}) %collective-permute-start.4) | collective-permute-done | bytes 655392 | tf_op jit(solution)/shard_map/ppermute | solution.py:228
  53.9 1.5 %collective-permute-start.8 = (bf16[256,1280]{1,0:T(8,128)(2,1)S(1)}, bf16[256,1280]{1,0:T(8,128)(2,1)S(1)}, u32[]{:S(2)}, u32[]{:S(2)}) collective-permute-start(bf16[256,1280]{1,0:T(8,128)(2,1)S(1)} %collective-permute-done.4.refs_0_), channel_id=1, source_target_pairs={{0,16},{4,20},{16,24},{20,28},{24,8},{28,12},{8,0},{12,4},{1,17},{... | collective-permute-start | bytes 1966088 | tf_op jit(solution)/shard_map/ppermute | solution.py:228
  55.4 0.5 collective-permute-start.1
  55.9 12.0 %collective-permute-done.6.refs_0_ = bf16[256,1280]{1,0:T(8,128)(2,1)S(1)} collective-permute-done((bf16[256,1280]{1,0:T(8,128)(2,1)S(1)}, bf16[256,1280]{1,0:T(8,128)(2,1)S(1)}, u32[]{:S(2)}, u32[]{:S(2)}) %collective-permute-start.6) | collective-permute-done | bytes 655392 | tf_op jit(solution)/shard_map/ppermute | solution.py:228
  67.9 1.5 %collective-permute-start.10 = (bf16[256,1280]{1,0:T(8,128)(2,1)S(1)}, bf16[256,1280]{1,0:T(8,128)(2,1)S(1)}, u32[]{:S(2)}, u32[]{:S(2)}) collective-permute-start(bf16[256,1280]{1,0:T(8,128)(2,1)S(1)} %collective-permute-done.6.refs_0_), channel_id=1, source_target_pairs={{0,16},{4,20},{16,24},{20,28},{24,8},{28,12},{8,0},{12,4},{1,17},{... | collective-permute-start | bytes 1966088 | tf_op jit(solution)/shard_map/ppermute | solution.py:228
  69.4 12.5 %collective-permute-done.8.refs_0_ = bf16[256,1280]{1,0:T(8,128)(2,1)S(1)} collective-permute-done((bf16[256,1280]{1,0:T(8,128)(2,1)S(1)}, bf16[256,1280]{1,0:T(8,128)(2,1)S(1)}, u32[]{:S(2)}, u32[]{:S(2)}) %collective-permute-start.8) | collective-permute-done | bytes 655392 | tf_op jit(solution)/shard_map/ppermute | solution.py:228
  82.0 1.5 %collective-permute-start.12 = (bf16[256,1280]{1,0:T(8,128)(2,1)S(1)}, bf16[256,1280]{1,0:T(8,128)(2,1)S(1)}, u32[]{:S(2)}, u32[]{:S(2)}) collective-permute-start(bf16[256,1280]{1,0:T(8,128)(2,1)S(1)} %collective-permute-done.8.refs_0_), channel_id=1, source_target_pairs={{0,16},{4,20},{16,24},{20,28},{24,8},{28,12},{8,0},{12,4},{1,17},{... | collective-permute-start | bytes 1966088 | tf_op jit(solution)/shard_map/ppermute | solution.py:228
  84.1 11.9 %collective-permute-done.10.refs_0_ = bf16[256,1280]{1,0:T(8,128)(2,1)S(1)} collective-permute-done((bf16[256,1280]{1,0:T(8,128)(2,1)S(1)}, bf16[256,1280]{1,0:T(8,128)(2,1)S(1)}, u32[]{:S(2)}, u32[]{:S(2)}) %collective-permute-start.10) | collective-permute-done | bytes 655392 | tf_op jit(solution)/shard_map/ppermute | solution.py:228
  96.0 12.8 %collective-permute-done.12.refs_0_ = bf16[256,1280]{1,0:T(8,128)(2,1)S(1)} collective-permute-done((bf16[256,1280]{1,0:T(8,128)(2,1)S(1)}, bf16[256,1280]{1,0:T(8,128)(2,1)S(1)}, u32[]{:S(2)}, u32[]{:S(2)}) %collective-permute-start.12) | collective-permute-done | bytes 655392 | tf_op jit(solution)/shard_map/ppermute | solution.py:228
  108.8 3.6 %write_pass.1 = (f32[512,1280]{1,0:T(8,128)}, f32[512,1280]{1,0:T(8,128)}, f32[512,1280]{1,0:T(8,128)}, bf16[4096,1280]{1,0:T(8,128)(2,1)}) custom-call(f32[32,2,128]{2,1,0:T(2,128)S(1)} %all_to_all.5.sums, f32[512,128]{1,0:T(8,128)S(1)} %get-tuple-element.15.member, f32[512,1280]{1,0:T(8,128)S(1)} %get-tuple-element.16.kept_master, ...), custom_call_target="tpu_custom_call" | custom-call | tf_op jit(solution)/shard_map/write_pass/pallas_call | solution.py:209
  112.4 1.1 place_pass.8.before
  113.5 1.1 place_pass.9.before
  114.6 1.1 place_pass.10.before
  115.8 1.1 place_pass.11.before
  116.9 1.1 place_pass.12.before
  118.0 1.1 place_pass.13.before
  119.2 0.9 place_pass.14.before
  120.1 0.9 place_pass.15
  (17 shorter events, 1.1 us)
Async XLA Ops:
  22.2 17.7 %collective-permute-start.2 = (bf16[256,1280]{1,0:T(8,128)(2,1)S(1)}, bf16[256,1280]{1,0:T(8,128)(2,1)S(1)}, u32[]{:S(2)}, u32[]{:S(2)}) collective-permute-start(bf16[256,1280]{1,0:T(8,128)(2,1)S(1)} %round_pass.2), channel_id=1, source_target_pairs={{0,16},{4,20},{16,24},{20,28},{24,8},{28,12},{8,0},{12,4},{1,17},{... | collective-permute-start | bytes 1966088 | tf_op jit(solution)/shard_map/ppermute | solution.py:228
  23.1 30.8 %collective-permute-start.4 = (bf16[256,1280]{1,0:T(8,128)(2,1)S(1)}, bf16[256,1280]{1,0:T(8,128)(2,1)S(1)}, u32[]{:S(2)}, u32[]{:S(2)}) collective-permute-start(bf16[256,1280]{1,0:T(8,128)(2,1)S(1)} %round_pass.3), channel_id=1, source_target_pairs={{0,16},{4,20},{16,24},{20,28},{24,8},{28,12},{8,0},{12,4},{1,17},{... | collective-permute-start | bytes 1966088 | tf_op jit(solution)/shard_map/ppermute | solution.py:228
  39.8 28.1 %collective-permute-start.6 = (bf16[256,1280]{1,0:T(8,128)(2,1)S(1)}, bf16[256,1280]{1,0:T(8,128)(2,1)S(1)}, u32[]{:S(2)}, u32[]{:S(2)}) collective-permute-start(bf16[256,1280]{1,0:T(8,128)(2,1)S(1)} %collective-permute-done.2.refs_0_), channel_id=1, source_target_pairs={{0,16},{4,20},{16,24},{20,28},{24,8},{28,12},{8,0},{12,4},{1,17},{... | collective-permute-start | bytes 1966088 | tf_op jit(solution)/shard_map/ppermute | solution.py:228
  53.9 28.1 %collective-permute-start.8 = (bf16[256,1280]{1,0:T(8,128)(2,1)S(1)}, bf16[256,1280]{1,0:T(8,128)(2,1)S(1)}, u32[]{:S(2)}, u32[]{:S(2)}) collective-permute-start(bf16[256,1280]{1,0:T(8,128)(2,1)S(1)} %collective-permute-done.4.refs_0_), channel_id=1, source_target_pairs={{0,16},{4,20},{16,24},{20,28},{24,8},{28,12},{8,0},{12,4},{1,17},{... | collective-permute-start | bytes 1966088 | tf_op jit(solution)/shard_map/ppermute | solution.py:228
  55.4 28.1 %collective-permute-start = (bf16[256,1280]{1,0:T(8,128)(2,1)S(1)}, bf16[256,1280]{1,0:T(8,128)(2,1)S(1)}, u32[]{:S(2)}, u32[]{:S(2)}) collective-permute-start(bf16[256,1280]{1,0:T(8,128)(2,1)S(1)} %round_pass.2), channel_id=1, source_target_pairs={{0,4},{4,0},{8,12},{12,8},{16,20},{20,16},{24,28},{28,24},{1,5},{5... | collective-permute-start | bytes 1966088 | tf_op jit(solution)/shard_map/ppermute | solution.py:229
  55.4 28.1 %collective-permute-start.1 = (bf16[256,1280]{1,0:T(8,128)(2,1)S(1)}, bf16[256,1280]{1,0:T(8,128)(2,1)S(1)}, u32[]{:S(2)}, u32[]{:S(2)}) collective-permute-start(bf16[256,1280]{1,0:T(8,128)(2,1)S(1)} %round_pass.3), channel_id=1, source_target_pairs={{0,4},{4,0},{8,12},{12,8},{16,20},{20,16},{24,28},{28,24},{1,5},{5... | collective-permute-start | bytes 1966088 | tf_op jit(solution)/shard_map/ppermute | solution.py:229
  55.9 28.1 %collective-permute-start.3 = (bf16[256,1280]{1,0:T(8,128)(2,1)S(1)}, bf16[256,1280]{1,0:T(8,128)(2,1)S(1)}, u32[]{:S(2)}, u32[]{:S(2)}) collective-permute-start(bf16[256,1280]{1,0:T(8,128)(2,1)S(1)} %collective-permute-done.2.refs_0_), channel_id=1, source_target_pairs={{0,4},{4,0},{8,12},{12,8},{16,20},{20,16},{24,28},{28,24},{1,5},{5... | collective-permute-start | bytes 1966088 | tf_op jit(solution)/shard_map/ppermute | solution.py:229
  67.9 28.1 %collective-permute-start.10 = (bf16[256,1280]{1,0:T(8,128)(2,1)S(1)}, bf16[256,1280]{1,0:T(8,128)(2,1)S(1)}, u32[]{:S(2)}, u32[]{:S(2)}) collective-permute-start(bf16[256,1280]{1,0:T(8,128)(2,1)S(1)} %collective-permute-done.6.refs_0_), channel_id=1, source_target_pairs={{0,16},{4,20},{16,24},{20,28},{24,8},{28,12},{8,0},{12,4},{1,17},{... | collective-permute-start | bytes 1966088 | tf_op jit(solution)/shard_map/ppermute | solution.py:228
  82.0 26.8 %collective-permute-start.12 = (bf16[256,1280]{1,0:T(8,128)(2,1)S(1)}, bf16[256,1280]{1,0:T(8,128)(2,1)S(1)}, u32[]{:S(2)}, u32[]{:S(2)}) collective-permute-start(bf16[256,1280]{1,0:T(8,128)(2,1)S(1)} %collective-permute-done.8.refs_0_), channel_id=1, source_target_pairs={{0,16},{4,20},{16,24},{20,28},{24,8},{28,12},{8,0},{12,4},{1,17},{... | collective-permute-start | bytes 1966088 | tf_op jit(solution)/shard_map/ppermute | solution.py:228
  83.5 31.2 %collective-permute-start.5 = (bf16[256,1280]{1,0:T(8,128)(2,1)S(1)}, bf16[256,1280]{1,0:T(8,128)(2,1)S(1)}, u32[]{:S(2)}, u32[]{:S(2)}) collective-permute-start(bf16[256,1280]{1,0:T(8,128)(2,1)S(1)} %collective-permute-done.4.refs_0_), channel_id=1, source_target_pairs={{0,4},{4,0},{8,12},{12,8},{16,20},{20,16},{24,28},{28,24},{1,5},{5... | collective-permute-start | bytes 1966088 | tf_op jit(solution)/shard_map/ppermute | solution.py:229
  83.5 32.3 %collective-permute-start.7 = (bf16[256,1280]{1,0:T(8,128)(2,1)S(1)}, bf16[256,1280]{1,0:T(8,128)(2,1)S(1)}, u32[]{:S(2)}, u32[]{:S(2)}) collective-permute-start(bf16[256,1280]{1,0:T(8,128)(2,1)S(1)} %collective-permute-done.6.refs_0_), channel_id=1, source_target_pairs={{0,4},{4,0},{8,12},{12,8},{16,20},{20,16},{24,28},{28,24},{1,5},{5... | collective-permute-start | bytes 1966088 | tf_op jit(solution)/shard_map/ppermute | solution.py:229
  84.0 32.9 %collective-permute-start.9 = (bf16[256,1280]{1,0:T(8,128)(2,1)S(1)}, bf16[256,1280]{1,0:T(8,128)(2,1)S(1)}, u32[]{:S(2)}, u32[]{:S(2)}) collective-permute-start(bf16[256,1280]{1,0:T(8,128)(2,1)S(1)} %collective-permute-done.8.refs_0_), channel_id=1, source_target_pairs={{0,4},{4,0},{8,12},{12,8},{16,20},{20,16},{24,28},{28,24},{1,5},{5... | collective-permute-start | bytes 1966088 | tf_op jit(solution)/shard_map/ppermute | solution.py:229
  96.0 22.0 %collective-permute-start.11 = (bf16[256,1280]{1,0:T(8,128)(2,1)S(1)}, bf16[256,1280]{1,0:T(8,128)(2,1)S(1)}, u32[]{:S(2)}, u32[]{:S(2)}) collective-permute-start(bf16[256,1280]{1,0:T(8,128)(2,1)S(1)} %collective-permute-done.10.refs_0_), channel_id=1, source_target_pairs={{0,4},{4,0},{8,12},{12,8},{16,20},{20,16},{24,28},{28,24},{1,5},{5... | collective-permute-start | bytes 1966088 | tf_op jit(solution)/shard_map/ppermute | solution.py:229
  108.8 11.3 %collective-permute-start.13 = (bf16[256,1280]{1,0:T(8,128)(2,1)S(1)}, bf16[256,1280]{1,0:T(8,128)(2,1)S(1)}, u32[]{:S(2)}, u32[]{:S(2)}) collective-permute-start(bf16[256,1280]{1,0:T(8,128)(2,1)S(1)} %collective-permute-done.12.refs_0_), channel_id=1, source_target_pairs={{0,4},{4,0},{8,12},{12,8},{16,20},{20,16},{24,28},{28,24},{1,5},{5... | collective-permute-start | bytes 1966088 | tf_op jit(solution)/shard_map/ppermute | solution.py:229

commit v2 on v1

v2 whole, which is shorter than its diff:
```python
import functools

import jax
import jax.numpy as jnp
from jax import lax
from jax.experimental import pallas as pl
from jax.experimental.pallas import tpu as pltpu
from jax.sharding import PartitionSpec as P


beta_first = 0.9
beta_second = 0.999
adam_epsilon = 1e-06
decay_rate = 0.3
learn_rate = 0.3
norm_epsilon = 1e-06

LANES = 128
TILE = 8
PIECE = 64
SHARES = (3, 1)
CHUNKS = len(SHARES)
MIB = 1024 * 1024
f32, bf16 = jnp.float32, jnp.bfloat16
hbm = pl.BlockSpec(memory_space=pltpu.HBM)
vmem = pl.BlockSpec(memory_space=pltpu.VMEM)


def in_hbm(*arrays):
    return tuple(pltpu.with_memory_space_constraint(a, pltpu.HBM) for a in arrays)


def power(base, steps):
    return lax.fori_loop(0, steps, lambda _, p: p * base, jnp.float32(1.0))


def piece_sizes(rows):
    return [PIECE] * (rows // PIECE - 1) + [PIECE // 2] * 2


def first_pass(step_count, rows_hbm, decay_hbm, master, moment_first, moment_second, gradients,
               kept_master, kept_first, kept_second, kept_grad, kept_update, member, sums,
               weight_rows, update_rows, mask_rows, tensor_rows, decay_mask, small_sems, sems):
    rows, cols = kept_master.shape
    small = []
    for a, (source, target) in enumerate(((rows_hbm, tensor_rows), (decay_hbm, decay_mask))):
        copy = pltpu.make_async_copy(source, target, small_sems.at[a])
        copy.start()
        small.append(copy)
    pieces, begin = [], 0
    for p, size in enumerate(piece_sizes(rows)):
        part = pl.ds(begin, size)
        copies = []
        for a, (source, target) in enumerate((
            (master, kept_master), (moment_first, kept_first), (moment_second, kept_second), (gradients, kept_grad),
        )):
            copies.append(pltpu.make_async_copy(source.at[part], target.at[part], sems.at[a, p]))
            copies[-1].start()
        pieces.append((begin, size, copies))
        begin += size
    for copy in small:
        copy.wait()

    steps = step_count[0]
    scale_first = 1.0 / (1.0 - jnp.full((TILE, LANES), power(jnp.float32(beta_first), steps)))
    scale_second = 1.0 / (1.0 - jnp.full((TILE, LANES), power(jnp.float32(beta_second), steps)))
    old_first, old_second = beta_first * scale_first, beta_second * scale_second
    add_first, add_second = (1.0 - beta_first) * scale_first, (1.0 - beta_second) * scale_second
    lane = lax.broadcasted_iota(jnp.int32, (TILE, LANES), 1)
    start = jnp.zeros((TILE, LANES), jnp.int32)
    end = jnp.zeros((TILE, LANES), jnp.int32)
    decay = jnp.zeros((TILE, LANES), f32)
    offset = jnp.int32(0)
    for k in range(tensor_rows.shape[0]):
        after = offset + tensor_rows[k]
        start = jnp.where(lane == k, offset, start)
        end = jnp.where(lane == k, after, end)
        decay = jnp.where(lane == k, decay_rate * decay_mask[k].astype(f32), decay)
        offset = after
    row = lax.axis_index("dp") * rows + lax.broadcasted_iota(jnp.int32, (TILE, LANES), 0)

    def belongs(i, carry):
        at = pl.ds(pl.multiple_of(i * TILE, TILE), TILE)
        here = row + i * TILE
        inside = jnp.where((here >= start) & (here < end), 1.0, 0.0)
        member[at] = inside
        mask_rows[at] = jnp.broadcast_to(jnp.sum(inside * decay, axis=1, keepdims=True), (TILE, LANES))
        return carry

    per_weight = jnp.zeros((TILE, LANES), f32)
    per_update = jnp.zeros((TILE, LANES), f32)
    for begin, size, copies in pieces:
        lax.fori_loop(begin // TILE, (begin + size) // TILE, belongs, 0, unroll=True)
        for copy in copies:
            copy.wait()

        def group(i, carry):
            at = pl.ds(pl.multiple_of(begin + i * TILE, TILE), TILE)
            mask = mask_rows[at]
            weight = jnp.zeros((TILE, LANES), f32)
            total = jnp.zeros((TILE, LANES), f32)
            for t in range(cols // LANES):
                tile = (at, pl.ds(t * LANES, LANES))
                grad = kept_grad[tile]
                value = kept_master[tile]
                top = old_first * kept_first[tile] + add_first * grad
                square = old_second * kept_second[tile] + add_second * grad * grad
                update = top * pl.reciprocal(square * lax.rsqrt(square) + adam_epsilon) + mask * value
                kept_update[tile] = update
                weight = weight + value * value
                total = total + update * update
            weight_rows[at] = weight
            update_rows[at] = total
            return carry

        lax.fori_loop(0, size // TILE, group, 0, unroll=4)
        for i in range(size // TILE):
            at = pl.ds(begin + i * TILE, TILE)
            inside = member[at]
            per_weight = per_weight + inside * jnp.sum(weight_rows[at], axis=1, keepdims=True)
            per_update = per_update + inside * jnp.sum(update_rows[at], axis=1, keepdims=True)

    both = jnp.concatenate(
        [jnp.sum(per_weight, axis=0, keepdims=True), jnp.sum(per_update, axis=0, keepdims=True)], axis=0
    )
    sums[...] = jnp.broadcast_to(both[None], sums.shape)


def rate_rows(sums, member):
    total = jnp.sum(sums[...], axis=0)
    ratio = jnp.sqrt(total[0:1]) / (jnp.sqrt(total[1:2]) + norm_epsilon)
    return jnp.sum(member * (learn_rate * ratio), axis=1, keepdims=True)


def round_pass(first, sums, member, kept_master, kept_update, chunk):
    part = pl.ds(first, chunk.shape[0])
    rate = rate_rows(sums, member[part])
    chunk[...] = (kept_master[part] - rate * kept_update[part]).astype(bf16)


def write_pass(sums, member, kept_master, kept_first, kept_second, kept_grad, kept_update,
               new_master, new_first, new_second, gathered, one, two, three, four, sems):
    rows = kept_master.shape[0]
    mine = pl.ds(pl.multiple_of(lax.axis_index("dp") * rows, rows), rows)
    copies = [
        pltpu.make_async_copy(source, target, sems.at[a]) for a, (source, target) in enumerate(
            ((one, new_first), (two, new_second), (three, new_master), (four, gathered.at[mine])))
    ]
    grad = kept_grad[...]
    one[...] = beta_first * kept_first[...] + (1.0 - beta_first) * grad
    copies[0].start()
    two[...] = beta_second * kept_second[...] + (1.0 - beta_second) * grad * grad
    copies[1].start()
    three[...] = kept_master[...] - rate_rows(sums, member[...]) * kept_update[...]
    copies[2].start()
    four[...] = three[...].astype(bf16)
    copies[3].start()
    for copy in copies:
        copy.wait()


def place_pass(chips, rows, items, before, *refs):
    pieces, (gathered, sems) = refs[:len(items)], refs[len(items):]
    me = lax.axis_index("dp")
    chip, core = me // 2, me % 2
    spot = jnp.where(chip % 2 == 0, chip // 2, chips - (chip + 1) // 2)
    copies = []
    for a, (step, swapped, first) in enumerate(items):
        at = (spot + chips - step) % chips
        source = jnp.where(2 * at < chips, 2 * at, 2 * (chips - at) - 1)
        owner = 2 * source + (1 - core if swapped else core)
        part = pl.ds(pl.multiple_of(owner * rows + first, 16), pieces[a].shape[0])
        copies.append(pltpu.make_async_copy(pieces[a], gathered.at[part], sems.at[a]))
        copies[-1].start()
    for copy in copies:
        copy.wait()


def place(chips, rows, items, gathered, *pieces):
    return pl.pallas_call(
        functools.partial(place_pass, chips, rows, items),
        out_shape=pltpu.HBM(gathered.shape, gathered.dtype),
        in_specs=[hbm] + [vmem] * len(items),
        out_specs=hbm,
        scratch_shapes=[pltpu.SemaphoreType.DMA((len(items),))],
        input_output_aliases={0: 0},
        compiler_params=pltpu.CompilerParams(vmem_limit_bytes=4 * MIB),
        name="place_pass",
    )(*in_hbm(gathered), *pieces)


def local(devices, dp, master, moment_first, moment_second, gradients, step_count, tensor_rows, decay_mask):
    rows, cols = master.shape
    kept = pltpu.VMEM((rows, cols), f32)
    small = [pltpu.SMEM(a.shape, a.dtype) for a in (tensor_rows, decay_mask)]

    kept_master, kept_first, kept_second, kept_grad, kept_update, member, sums = pl.pallas_call(
        first_pass,
        out_shape=(kept,) * 5 + (pltpu.VMEM((rows, LANES), f32), jax.ShapeDtypeStruct((devices, 2, LANES), f32)),
        in_specs=[pl.BlockSpec(memory_space=pltpu.SMEM)] + [hbm] * 6,
        out_specs=(vmem,) * 7,
        scratch_shapes=[pltpu.VMEM((rows, LANES), f32)] * 3 + small
        + [pltpu.SemaphoreType.DMA((2,)), pltpu.SemaphoreType.DMA((4, len(piece_sizes(rows))))],
        compiler_params=pltpu.CompilerParams(vmem_limit_bytes=4 * MIB),
        name="first_pass",
    )(step_count, *in_hbm(tensor_rows, decay_mask, master, moment_first, moment_second, gradients))

    sums = lax.all_to_all(sums, ("dp", "mp"), 0, 0, tiled=True)

    sizes = [rows * share // sum(SHARES) for share in SHARES]
    firsts = [sum(sizes[:i]) for i in range(CHUNKS)]
    pieces = []
    for i in range(CHUNKS):
        pieces.append(pl.pallas_call(
            functools.partial(round_pass, firsts[i]),
            out_shape=pltpu.VMEM((sizes[i], cols), bf16),
            in_specs=[vmem] * 4,
            out_specs=vmem,
            compiler_params=pltpu.CompilerParams(vmem_limit_bytes=4 * MIB),
            name="round_pass",
        )(sums, member, kept_master, kept_update))

    new_master, new_first, new_second, gathered = pl.pallas_call(
        write_pass,
        out_shape=(jax.ShapeDtypeStruct((rows, cols), f32),) * 3 + (pltpu.HBM((dp * rows, cols), bf16),),
        in_specs=[vmem] * 7,
        out_specs=(hbm,) * 4,
        scratch_shapes=[pltpu.VMEM((rows, cols), f32)] * 3 + [pltpu.VMEM((rows, cols), bf16), pltpu.SemaphoreType.DMA((4,))],
        compiler_params=pltpu.CompilerParams(vmem_limit_bytes=24 * MIB),
        name="write_pass",
    )(sums, member, kept_master, kept_first, kept_second, kept_grad, kept_update)

    chips = dp // 2
    order = [2 * p if 2 * p < chips else 2 * (chips - p) - 1 for p in range(chips)]
    ring = [(2 * order[p] + c, 2 * order[(p + 1) % chips] + c) for p in range(chips) for c in range(2)]
    partner = [(d, d ^ 1) for d in range(dp)]
    others = []
    for k in range(chips):
        for i in range(CHUNKS):
            piece, first = pieces[i], firsts[i]
            if k < chips - 1:
                pieces[i] = lax.ppermute(piece, "dp", ring)
            other = lax.ppermute(piece, "dp", partner)
            if k == 0:
                others.append(other)
                if i == CHUNKS - 1:
                    gathered = place(chips, rows, tuple((0, True, first) for first in firsts), gathered, *others)
            elif k == chips - 1 and i == CHUNKS - 1:
                gathered = place(chips, rows, ((k, False, first),), gathered, piece)
                gathered = place(chips, rows, ((k, True, first),), gathered, other)
            else:
                gathered = place(chips, rows, ((k, False, first), (k, True, first)), gathered, piece, other)
    return new_master, new_first, new_second, gathered


def solution(mesh):
    placed = (P("dp", "mp"), P("dp", "mp"), P("dp", "mp"), P("dp", "mp"), P(), P(), P())
    body = functools.partial(local, mesh.size, mesh.shape["dp"])

    return jax.shard_map(
        body,
        mesh=mesh,
        in_specs=placed,
        out_specs=(P("dp", "mp"), P("dp", "mp"), P("dp", "mp"), P(None, "mp")),
        check_vma=False,
    )
```

time: 121 us -> 126 us (1.041)
  starting transfers between devices: 8.43 us -> 12.2 us
  waiting for transfers between devices: 77.9 us -> 79.6 us
    ppermute x6, starting transfers between devices: 7.34 us -> 10.5 us  [local(): pieces[i] = lax.ppermute(piece, 'dp', ring)]
    ppermute x6, waiting for transfers between devices: 77.9 us -> 79.5 us  [local(): pieces[i] = lax.ppermute(piece, 'dp', ring)]
    pallas_call x3, Pallas kernels: 6.68 us -> 5.18 us  [the longest x1 4.7 us: local(): pl.pallas_call(first_pass, out_shape=(kept,) * 5 + (pltpu.VMEM((rows, LAN...]
  transfers between devices with their start and end apart: 14 -> 14, of which waited for: 6 -> 5; matrix products, arithmetic and copies ran while one was open for 0% -> 0% of each run, Pallas kernels for 9% -> 10%
where the time goes in v2:
time: 126 us
  waiting for transfers between devices  79.6 us (63%)
  Pallas kernels  18.1 us (14%)
  blocking collectives  14.4 us (11%)
  starting transfers between devices  12.2 us (10%)
  between operations  1.43 us (1%)
    ppermute x6, waiting for transfers between devices, local(): pieces[i] = lax.ppermute(piece, 'dp', ring)  79.5 us
    all_to_all x1, blocking collectives, local(): sums = lax.all_to_all(sums, ('dp', 'mp'), 0, 0, tiled=True)  14.4 us
    ppermute x6, starting transfers between devices, local(): pieces[i] = lax.ppermute(piece, 'dp', ring)  10.5 us
    pallas_call x8, Pallas kernels, place(): pl.pallas_call(functools.partial(place_pass, chips, rows, items), out_sha...  8.41 us
    pallas_call x1, Pallas kernels, local(): pl.pallas_call(first_pass, out_shape=(kept,) * 5 + (pltpu.VMEM((rows, LAN...  4.7 us
    pallas_call x1, Pallas kernels, local(): pl.pallas_call(write_pass, out_shape=(jax.ShapeDtypeStruct((rows, cols),...  4.52 us
  transfers between devices with their start and end apart: 14, of which 5 were waited for; matrix products, arithmetic and copies ran while one was open for 0% of the time, Pallas kernels for 10%

profile of v2, /device:TPU:0, one launch (start us, length us, event | category | flops | bytes accessed | tf_op | source)
XLA Modules:
  0.0 125.7 jit_solution(15522434821189715701)
XLA Ops:
  1.3 4.7 %first_pass.1 = (f32[512,1280]{1,0:T(8,128)S(1)}, f32[512,1280]{1,0:T(8,128)S(1)}, f32[512,1280]{1,0:T(8,128)S(1)}, f32[512,1280]{1,0:T(8,128)S(1)}, f32[512,128...) custom-call(s32[1]{0:T(128)S(6)} %copy.27.step_count, s32[24]{0:T(128)} %rows_hbm.1, s32[24]{0:T(128)} %decay_hbm.1, ...), custom_call_target="tpu_custom_call" | custom-call | tf_op jit(solution)/shard_map/first_pass/pallas_call | solution.py:197
  6.0 14.4 %all_to_all.5.sums = f32[32,2,128]{2,1,0:T(2,128)S(1)} all-to-all(f32[32,2,128]{2,1,0:T(2,128)S(1)} %get-tuple-element.15), channel_id=1, replica_groups=mesh['dp'=8,'mp'=4] {'dp','mp'}, dimensions={0} | all-to-all | bytes 65536 | tf_op jit(solution)/shard_map/all_to_all | solution.py:208
  20.7 0.7 collective-permute-start.2
  21.4 22.7 %collective-permute-done.2.refs_0_ = bf16[384,1280]{1,0:T(8,128)(2,1)S(1)} collective-permute-done((bf16[384,1280]{1,0:T(8,128)(2,1)S(1)}, bf16[384,1280]{1,0:T(8,128)(2,1)S(1)}, u32[]{:S(2)}, u32[]{:S(2)}) %collective-permute-start.2) | collective-permute-done | bytes 983072 | tf_op jit(solution)/shard_map/ppermute | solution.py:242
  44.1 1.5 %collective-permute-start.6 = (bf16[384,1280]{1,0:T(8,128)(2,1)S(1)}, bf16[384,1280]{1,0:T(8,128)(2,1)S(1)}, u32[]{:S(2)}, u32[]{:S(2)}) collective-permute-start(bf16[384,1280]{1,0:T(8,128)(2,1)S(1)} %collective-permute-done.2.refs_0_), channel_id=1, source_target_pairs={{0,16},{4,20},{16,24},{20,28},{24,8},{28,12},{8,0},{12,4},{1,17},{... | collective-permute-start | bytes 2949128 | tf_op jit(solution)/shard_map/ppermute | solution.py:242
  45.6 21.0 %collective-permute-done.6.refs_0_ = bf16[384,1280]{1,0:T(8,128)(2,1)S(1)} collective-permute-done((bf16[384,1280]{1,0:T(8,128)(2,1)S(1)}, bf16[384,1280]{1,0:T(8,128)(2,1)S(1)}, u32[]{:S(2)}, u32[]{:S(2)}) %collective-permute-start.6) | collective-permute-done | bytes 983072 | tf_op jit(solution)/shard_map/ppermute | solution.py:242
  66.6 2.4 %collective-permute-start.10 = (bf16[384,1280]{1,0:T(8,128)(2,1)S(1)}, bf16[384,1280]{1,0:T(8,128)(2,1)S(1)}, u32[]{:S(2)}, u32[]{:S(2)}) collective-permute-start(bf16[384,1280]{1,0:T(8,128)(2,1)S(1)} %collective-permute-done.6.refs_0_), channel_id=1, source_target_pairs={{0,16},{4,20},{16,24},{20,28},{24,8},{28,12},{8,0},{12,4},{1,17},{... | collective-permute-start | bytes 2949128 | tf_op jit(solution)/shard_map/ppermute | solution.py:242
  69.3 0.6 collective-permute-start.1
  69.9 26.0 %collective-permute-done.4.refs_0_ = bf16[128,1280]{1,0:T(8,128)(2,1)S(1)} collective-permute-done((bf16[128,1280]{1,0:T(8,128)(2,1)S(1)}, bf16[128,1280]{1,0:T(8,128)(2,1)S(1)}, u32[]{:S(2)}, u32[]{:S(2)}) %collective-permute-start.4) | collective-permute-done | bytes 327712 | tf_op jit(solution)/shard_map/ppermute | solution.py:242
  95.9 2.6 %collective-permute-start.8 = (bf16[128,1280]{1,0:T(8,128)(2,1)S(1)}, bf16[128,1280]{1,0:T(8,128)(2,1)S(1)}, u32[]{:S(2)}, u32[]{:S(2)}) collective-permute-start(bf16[128,1280]{1,0:T(8,128)(2,1)S(1)} %collective-permute-done.4.refs_0_), channel_id=1, source_target_pairs={{0,16},{4,20},{16,24},{20,28},{24,8},{28,12},{8,0},{12,4},{1,17},{... | collective-permute-start | bytes 983048 | tf_op jit(solution)/shard_map/ppermute | solution.py:242
  98.6 0.5 collective-permute-start.11
  99.1 4.8 %collective-permute-done.8.refs_0_ = bf16[128,1280]{1,0:T(8,128)(2,1)S(1)} collective-permute-done((bf16[128,1280]{1,0:T(8,128)(2,1)S(1)}, bf16[128,1280]{1,0:T(8,128)(2,1)S(1)}, u32[]{:S(2)}, u32[]{:S(2)}) %collective-permute-start.8) | collective-permute-done | bytes 327712 | tf_op jit(solution)/shard_map/ppermute | solution.py:242
  103.9 3.2 %collective-permute-start.12 = (bf16[128,1280]{1,0:T(8,128)(2,1)S(1)}, bf16[128,1280]{1,0:T(8,128)(2,1)S(1)}, u32[]{:S(2)}, u32[]{:S(2)}) collective-permute-start(bf16[128,1280]{1,0:T(8,128)(2,1)S(1)} %collective-permute-done.8.refs_0_), channel_id=1, source_target_pairs={{0,16},{4,20},{16,24},{20,28},{24,8},{28,12},{8,0},{12,4},{1,17},{... | collective-permute-start | bytes 983048 | tf_op jit(solution)/shard_map/ppermute | solution.py:242
  107.1 5.0 %collective-permute-done.12.refs_0_ = bf16[128,1280]{1,0:T(8,128)(2,1)S(1)} collective-permute-done((bf16[128,1280]{1,0:T(8,128)(2,1)S(1)}, bf16[128,1280]{1,0:T(8,128)(2,1)S(1)}, u32[]{:S(2)}, u32[]{:S(2)}) %collective-permute-start.12) | collective-permute-done | bytes 327712 | tf_op jit(solution)/shard_map/ppermute | solution.py:242
  112.1 0.5 collective-permute-start.13
  112.7 4.5 %write_pass.1 = (f32[512,1280]{1,0:T(8,128)}, f32[512,1280]{1,0:T(8,128)}, f32[512,1280]{1,0:T(8,128)}, bf16[4096,1280]{1,0:T(8,128)(2,1)}) custom-call(f32[32,2,128]{2,1,0:T(2,128)S(1)} %all_to_all.5.sums, f32[512,128]{1,0:T(8,128)S(1)} %get-tuple-element.16.member, f32[512,1280]{1,0:T(8,128)S(1)} %get-tuple-element.17.kept_master, ...), custom_call_target="tpu_custom_call" | custom-call | tf_op jit(solution)/shard_map/write_pass/pallas_call | solution.py:223
  117.2 1.1 place_pass.8.before
  118.3 1.3 %place_pass.9.before = bf16[4096,1280]{1,0:T(8,128)(2,1)} custom-call(bf16[4096,1280]{1,0:T(8,128)(2,1)} %place_pass.8.before, bf16[384,1280]{1,0:T(8,128)(2,1)S(1)} %collective-permute-done.2.refs_0_, bf16[384,1280]{1,0:T(8,128)(2,1)S(1)} %collective-permute-done.3.refs_1_), custom_call_target="tpu_custom_call", output_to_operand_aliasing={{}: (0, {})} | custom-call | tf_op jit(solution)/shard_map/place_pass/pallas_call | solution.py:180
  119.6 0.9 place_pass.10.before
  120.5 1.3 %place_pass.11.before = bf16[4096,1280]{1,0:T(8,128)(2,1)} custom-call(bf16[4096,1280]{1,0:T(8,128)(2,1)} %place_pass.10.before, bf16[384,1280]{1,0:T(8,128)(2,1)S(1)} %collective-permute-done.6.refs_0_, bf16[384,1280]{1,0:T(8,128)(2,1)S(1)} %collective-permute-done.7.refs_1_), custom_call_target="tpu_custom_call", output_to_operand_aliasing={{}: (0, {})} | custom-call | tf_op jit(solution)/shard_map/place_pass/pallas_call | solution.py:180
  121.9 0.9 place_pass.12.before
  122.8 1.3 %place_pass.13.before = bf16[4096,1280]{1,0:T(8,128)(2,1)} custom-call(bf16[4096,1280]{1,0:T(8,128)(2,1)} %place_pass.12.before, bf16[384,1280]{1,0:T(8,128)(2,1)S(1)} %collective-permute-done.10.refs_0_, bf16[384,1280]{1,0:T(8,128)(2,1)S(1)} %collective-permute-done.11.refs_1_), custom_call_target="tpu_custom_call", output_to_operand_aliasing={{}: (0, {})} | custom-call | tf_op jit(solution)/shard_map/place_pass/pallas_call | solution.py:180
  124.1 0.8 place_pass.14.before
  124.9 0.8 place_pass.15
  (17 shorter events, 0.6 us)
Async XLA Ops:
  20.7 23.4 %collective-permute-start.2 = (bf16[384,1280]{1,0:T(8,128)(2,1)S(1)}, bf16[384,1280]{1,0:T(8,128)(2,1)S(1)}, u32[]{:S(2)}, u32[]{:S(2)}) collective-permute-start(bf16[384,1280]{1,0:T(8,128)(2,1)S(1)} %round_pass.2), channel_id=1, source_target_pairs={{0,16},{4,20},{16,24},{20,28},{24,8},{28,12},{8,0},{12,4},{1,17},{... | collective-permute-start | bytes 2949128 | tf_op jit(solution)/shard_map/ppermute | solution.py:242
  44.1 22.5 %collective-permute-start.6 = (bf16[384,1280]{1,0:T(8,128)(2,1)S(1)}, bf16[384,1280]{1,0:T(8,128)(2,1)S(1)}, u32[]{:S(2)}, u32[]{:S(2)}) collective-permute-start(bf16[384,1280]{1,0:T(8,128)(2,1)S(1)} %collective-permute-done.2.refs_0_), channel_id=1, source_target_pairs={{0,16},{4,20},{16,24},{20,28},{24,8},{28,12},{8,0},{12,4},{1,17},{... | collective-permute-start | bytes 2949128 | tf_op jit(solution)/shard_map/ppermute | solution.py:242
  66.6 32.0 %collective-permute-start.10 = (bf16[384,1280]{1,0:T(8,128)(2,1)S(1)}, bf16[384,1280]{1,0:T(8,128)(2,1)S(1)}, u32[]{:S(2)}, u32[]{:S(2)}) collective-permute-start(bf16[384,1280]{1,0:T(8,128)(2,1)S(1)} %collective-permute-done.6.refs_0_), channel_id=1, source_target_pairs={{0,16},{4,20},{16,24},{20,28},{24,8},{28,12},{8,0},{12,4},{1,17},{... | collective-permute-start | bytes 2949128 | tf_op jit(solution)/shard_map/ppermute | solution.py:242
  69.0 38.1 %collective-permute-start = (bf16[384,1280]{1,0:T(8,128)(2,1)S(1)}, bf16[384,1280]{1,0:T(8,128)(2,1)S(1)}, u32[]{:S(2)}, u32[]{:S(2)}) collective-permute-start(bf16[384,1280]{1,0:T(8,128)(2,1)S(1)} %round_pass.2), channel_id=1, source_target_pairs={{0,4},{4,0},{8,12},{12,8},{16,20},{20,16},{24,28},{28,24},{1,5},{5... | collective-permute-start | bytes 2949128 | tf_op jit(solution)/shard_map/ppermute | solution.py:243
  69.2 26.7 %collective-permute-start.4 = (bf16[128,1280]{1,0:T(8,128)(2,1)S(1)}, bf16[128,1280]{1,0:T(8,128)(2,1)S(1)}, u32[]{:S(2)}, u32[]{:S(2)}) collective-permute-start(bf16[128,1280]{1,0:T(8,128)(2,1)S(1)} %round_pass.3), channel_id=1, source_target_pairs={{0,16},{4,20},{16,24},{20,28},{24,8},{28,12},{8,0},{12,4},{1,17},{... | collective-permute-start | bytes 983048 | tf_op jit(solution)/shard_map/ppermute | solution.py:242
  69.3 29.3 %collective-permute-start.1 = (bf16[128,1280]{1,0:T(8,128)(2,1)S(1)}, bf16[128,1280]{1,0:T(8,128)(2,1)S(1)}, u32[]{:S(2)}, u32[]{:S(2)}) collective-permute-start(bf16[128,1280]{1,0:T(8,128)(2,1)S(1)} %round_pass.3), channel_id=1, source_target_pairs={{0,4},{4,0},{8,12},{12,8},{16,20},{20,16},{24,28},{28,24},{1,5},{5... | collective-permute-start | bytes 983048 | tf_op jit(solution)/shard_map/ppermute | solution.py:243
  69.9 42.3 %collective-permute-start.3 = (bf16[384,1280]{1,0:T(8,128)(2,1)S(1)}, bf16[384,1280]{1,0:T(8,128)(2,1)S(1)}, u32[]{:S(2)}, u32[]{:S(2)}) collective-permute-start(bf16[384,1280]{1,0:T(8,128)(2,1)S(1)} %collective-permute-done.2.refs_0_), channel_id=1, source_target_pairs={{0,4},{4,0},{8,12},{12,8},{16,20},{20,16},{24,28},{28,24},{1,5},{5... | collective-permute-start | bytes 2949128 | tf_op jit(solution)/shard_map/ppermute | solution.py:243
  95.9 7.9 %collective-permute-start.8 = (bf16[128,1280]{1,0:T(8,128)(2,1)S(1)}, bf16[128,1280]{1,0:T(8,128)(2,1)S(1)}, u32[]{:S(2)}, u32[]{:S(2)}) collective-permute-start(bf16[128,1280]{1,0:T(8,128)(2,1)S(1)} %collective-permute-done.4.refs_0_), channel_id=1, source_target_pairs={{0,16},{4,20},{16,24},{20,28},{24,8},{28,12},{8,0},{12,4},{1,17},{... | collective-permute-start | bytes 983048 | tf_op jit(solution)/shard_map/ppermute | solution.py:242
  98.6 21.9 %collective-permute-start.7 = (bf16[384,1280]{1,0:T(8,128)(2,1)S(1)}, bf16[384,1280]{1,0:T(8,128)(2,1)S(1)}, u32[]{:S(2)}, u32[]{:S(2)}) collective-permute-start(bf16[384,1280]{1,0:T(8,128)(2,1)S(1)} %collective-permute-done.6.refs_0_), channel_id=1, source_target_pairs={{0,4},{4,0},{8,12},{12,8},{16,20},{20,16},{24,28},{28,24},{1,5},{5... | collective-permute-start | bytes 2949128 | tf_op jit(solution)/shard_map/ppermute | solution.py:243
  98.6 24.2 %collective-permute-start.11 = (bf16[384,1280]{1,0:T(8,128)(2,1)S(1)}, bf16[384,1280]{1,0:T(8,128)(2,1)S(1)}, u32[]{:S(2)}, u32[]{:S(2)}) collective-permute-start(bf16[384,1280]{1,0:T(8,128)(2,1)S(1)} %collective-permute-done.10.refs_0_), channel_id=1, source_target_pairs={{0,4},{4,0},{8,12},{12,8},{16,20},{20,16},{24,28},{28,24},{1,5},{5... | collective-permute-start | bytes 2949128 | tf_op jit(solution)/shard_map/ppermute | solution.py:243
  103.9 8.3 %collective-permute-start.12 = (bf16[128,1280]{1,0:T(8,128)(2,1)S(1)}, bf16[128,1280]{1,0:T(8,128)(2,1)S(1)}, u32[]{:S(2)}, u32[]{:S(2)}) collective-permute-start(bf16[128,1280]{1,0:T(8,128)(2,1)S(1)} %collective-permute-done.8.refs_0_), channel_id=1, source_target_pairs={{0,16},{4,20},{16,24},{20,28},{24,8},{28,12},{8,0},{12,4},{1,17},{... | collective-permute-start | bytes 983048 | tf_op jit(solution)/shard_map/ppermute | solution.py:242
  107.1 12.5 %collective-permute-start.5 = (bf16[128,1280]{1,0:T(8,128)(2,1)S(1)}, bf16[128,1280]{1,0:T(8,128)(2,1)S(1)}, u32[]{:S(2)}, u32[]{:S(2)}) collective-permute-start(bf16[128,1280]{1,0:T(8,128)(2,1)S(1)} %collective-permute-done.4.refs_0_), channel_id=1, source_target_pairs={{0,4},{4,0},{8,12},{12,8},{16,20},{20,16},{24,28},{28,24},{1,5},{5... | collective-permute-start | bytes 983048 | tf_op jit(solution)/shard_map/ppermute | solution.py:243
  112.1 9.7 %collective-permute-start.9 = (bf16[128,1280]{1,0:T(8,128)(2,1)S(1)}, bf16[128,1280]{1,0:T(8,128)(2,1)S(1)}, u32[]{:S(2)}, u32[]{:S(2)}) collective-permute-start(bf16[128,1280]{1,0:T(8,128)(2,1)S(1)} %collective-permute-done.8.refs_0_), channel_id=1, source_target_pairs={{0,4},{4,0},{8,12},{12,8},{16,20},{20,16},{24,28},{28,24},{1,5},{5... | collective-permute-start | bytes 983048 | tf_op jit(solution)/shard_map/ppermute | solution.py:243
  112.1 12.8 %collective-permute-start.13 = (bf16[128,1280]{1,0:T(8,128)(2,1)S(1)}, bf16[128,1280]{1,0:T(8,128)(2,1)S(1)}, u32[]{:S(2)}, u32[]{:S(2)}) collective-permute-start(bf16[128,1280]{1,0:T(8,128)(2,1)S(1)} %collective-permute-done.12.refs_0_), channel_id=1, source_target_pairs={{0,4},{4,0},{8,12},{12,8},{16,20},{20,16},{24,28},{28,24},{1,5},{5... | collective-permute-start | bytes 983048 | tf_op jit(solution)/shard_map/ppermute | solution.py:243

commit v3 on v2

--- a/solution.py
+++ b/solution.py
@@ -20,6 +20,7 @@
 PIECE = 64
 SHARES = (3, 1)
 CHUNKS = len(SHARES)
+EARLY = 16
 MIB = 1024 * 1024
 f32, bf16 = jnp.float32, jnp.bfloat16
 hbm = pl.BlockSpec(memory_space=pltpu.HBM)
@@ -39,7 +40,7 @@
 
 
 def first_pass(step_count, rows_hbm, decay_hbm, master, moment_first, moment_second, gradients,
-               kept_master, kept_first, kept_second, kept_grad, kept_update, member, sums,
+               kept_master, kept_first, kept_second, kept_grad, kept_update, member, bounds, pair, sums,
                weight_rows, update_rows, mask_rows, tensor_rows, decay_mask, small_sems, sems):
     rows, cols = kept_master.shape
     small = []
@@ -77,6 +78,8 @@
         end = jnp.where(lane == k, after, end)
         decay = jnp.where(lane == k, decay_rate * decay_mask[k].astype(f32), decay)
         offset = after
+    bounds[0] = start
+    bounds[1] = end
     row = lax.axis_index("dp") * rows + lax.broadcasted_iota(jnp.int32, (TILE, LANES), 0)
 
     def belongs(i, carry):
@@ -120,6 +123,9 @@
             per_weight = per_weight + inside * jnp.sum(weight_rows[at], axis=1, keepdims=True)
             per_update = per_update + inside * jnp.sum(update_rows[at], axis=1, keepdims=True)
 
+    early = pair.shape[1]
+    pair[0] = kept_master[pl.ds(rows - early, early)]
+    pair[1] = kept_update[pl.ds(rows - early, early)]
     both = jnp.concatenate(
         [jnp.sum(per_weight, axis=0, keepdims=True), jnp.sum(per_update, axis=0, keepdims=True)], axis=0
     )
@@ -132,10 +138,28 @@
     return jnp.sum(member * (learn_rate * ratio), axis=1, keepdims=True)
 
 
-def round_pass(first, sums, member, kept_master, kept_update, chunk):
-    part = pl.ds(first, chunk.shape[0])
+def round_pass(first, sums, member, kept_master, kept_update, *chunks):
+    part = pl.ds(first, chunks[0].shape[0])
     rate = rate_rows(sums, member[part])
-    chunk[...] = (kept_master[part] - rate * kept_update[part]).astype(bf16)
+    values = (kept_master[part] - rate * kept_update[part]).astype(bf16)
+    for chunk in chunks:
+        chunk[...] = values[:chunk.shape[0]]
+
+
+def ring_owner(chips, step):
+    chip = lax.axis_index("dp") // 2
+    spot = jnp.where(chip % 2 == 0, chip // 2, chips - (chip + 1) // 2)
+    at = (spot + chips - step) % chips
+    return jnp.where(2 * at < chips, 2 * at, 2 * (chips - at) - 1)
+
+
+def merge_pass(chips, rows, sums, bounds, short, pair, chunk):
+    early = pair.shape[1]
+    owner = 2 * ring_owner(chips, 1) + lax.axis_index("dp") % 2
+    row = owner * rows + rows - early + lax.broadcasted_iota(jnp.int32, (early, LANES), 0)
+    member = jnp.where((row >= bounds[0, 0:1]) & (row < bounds[1, 0:1]), 1.0, 0.0)
+    chunk[pl.ds(0, short.shape[0])] = short[...]
+    chunk[pl.ds(short.shape[0], early)] = (pair[0] - rate_rows(sums, member) * pair[1]).astype(bf16)
 
 
 def write_pass(sums, member, kept_master, kept_first, kept_second, kept_grad, kept_update,
@@ -161,14 +185,10 @@
 
 def place_pass(chips, rows, items, before, *refs):
     pieces, (gathered, sems) = refs[:len(items)], refs[len(items):]
-    me = lax.axis_index("dp")
-    chip, core = me // 2, me % 2
-    spot = jnp.where(chip % 2 == 0, chip // 2, chips - (chip + 1) // 2)
+    core = lax.axis_index("dp") % 2
     copies = []
     for a, (step, swapped, first) in enumerate(items):
-        at = (spot + chips - step) % chips
-        source = jnp.where(2 * at < chips, 2 * at, 2 * (chips - at) - 1)
-        owner = 2 * source + (1 - core if swapped else core)
+        owner = 2 * ring_owner(chips, step) + (1 - core if swapped else core)
         part = pl.ds(pl.multiple_of(owner * rows + first, 16), pieces[a].shape[0])
         copies.append(pltpu.make_async_copy(pieces[a], gathered.at[part], sems.at[a]))
         copies[-1].start()
@@ -192,30 +212,39 @@
 def local(devices, dp, master, moment_first, moment_second, gradients, step_count, tensor_rows, decay_mask):
     rows, cols = master.shape
     kept = pltpu.VMEM((rows, cols), f32)
+    early = rows // EARLY
+    chips = dp // 2
+    order = [2 * p if 2 * p < chips else 2 * (chips - p) - 1 for p in range(chips)]
+    ring = [(2 * order[p] + c, 2 * order[(p + 1) % chips] + c) for p in range(chips) for c in range(2)]
+    partner = [(d, d ^ 1) for d in range(dp)]
     small = [pltpu.SMEM(a.shape, a.dtype) for a in (tensor_rows, decay_mask)]
 
-    kept_master, kept_first, kept_second, kept_grad, kept_update, member, sums = pl.pallas_call(
+    kept_master, kept_first, kept_second, kept_grad, kept_update, member, bounds, pair, sums = pl.pallas_call(
         first_pass,
-        out_shape=(kept,) * 5 + (pltpu.VMEM((rows, LANES), f32), jax.ShapeDtypeStruct((devices, 2, LANES), f32)),
+        out_shape=(kept,) * 5 + (
+            pltpu.VMEM((rows, LANES), f32), pltpu.VMEM((2, TILE, LANES), jnp.int32), pltpu.VMEM((2, early, cols), f32),
+            jax.ShapeDtypeStruct((devices, 2, LANES), f32)),
         in_specs=[pl.BlockSpec(memory_space=pltpu.SMEM)] + [hbm] * 6,
-        out_specs=(vmem,) * 7,
+        out_specs=(vmem,) * 9,
         scratch_shapes=[pltpu.VMEM((rows, LANES), f32)] * 3 + small
         + [pltpu.SemaphoreType.DMA((2,)), pltpu.SemaphoreType.DMA((4, len(piece_sizes(rows))))],
         compiler_params=pltpu.CompilerParams(vmem_limit_bytes=4 * MIB),
         name="first_pass",
     )(step_count, *in_hbm(tensor_rows, decay_mask, master, moment_first, moment_second, gradients))
 
+    pair = lax.ppermute(pair, "dp", ring)
     sums = lax.all_to_all(sums, ("dp", "mp"), 0, 0, tiled=True)
 
     sizes = [rows * share // sum(SHARES) for share in SHARES]
     firsts = [sum(sizes[:i]) for i in range(CHUNKS)]
     pieces = []
     for i in range(CHUNKS):
+        shapes = (sizes[i],) if i < CHUNKS - 1 else (sizes[i], sizes[i] - early)
         pieces.append(pl.pallas_call(
             functools.partial(round_pass, firsts[i]),
-            out_shape=pltpu.VMEM((sizes[i], cols), bf16),
+            out_shape=tuple(pltpu.VMEM((size, cols), bf16) for size in shapes),
             in_specs=[vmem] * 4,
-            out_specs=vmem,
+            out_specs=(vmem,) * len(shapes),
             compiler_params=pltpu.CompilerParams(vmem_limit_bytes=4 * MIB),
             name="round_pass",
         )(sums, member, kept_master, kept_update))
@@ -230,16 +259,23 @@
         name="write_pass",
     )(sums, member, kept_master, kept_first, kept_second, kept_grad, kept_update)
 
-    chips = dp // 2
-    order = [2 * p if 2 * p < chips else 2 * (chips - p) - 1 for p in range(chips)]
-    ring = [(2 * order[p] + c, 2 * order[(p + 1) % chips] + c) for p in range(chips) for c in range(2)]
-    partner = [(d, d ^ 1) for d in range(dp)]
+    short = pieces[-1][1]
+    pieces = [piece[0] for piece in pieces]
     others = []
     for k in range(chips):
         for i in range(CHUNKS):
             piece, first = pieces[i], firsts[i]
             if k < chips - 1:
-                pieces[i] = lax.ppermute(piece, "dp", ring)
+                pieces[i] = lax.ppermute(short if (k, i) == (0, CHUNKS - 1) else piece, "dp", ring)
+                if (k, i) == (0, CHUNKS - 1):
+                    pieces[i] = pl.pallas_call(
+                        functools.partial(merge_pass, chips, rows),
+                        out_shape=pltpu.VMEM((sizes[i], cols), bf16),
+                        in_specs=[vmem] * 4,
+                        out_specs=vmem,
+                        compiler_params=pltpu.CompilerParams(vmem_limit_bytes=4 * MIB),
+                        name="merge_pass",
+                    )(sums, bounds, pieces[i], pair)
             other = lax.ppermute(piece, "dp", partner)
             if k == 0:
                 others.append(other)

time: 126 us -> 132 us (1.048)
  starting transfers between devices: 12.2 us -> 15 us
  waiting for transfers between devices: 79.6 us -> 82.1 us
    ppermute x6 -> x7, starting transfers between devices: 10.5 us -> 13.4 us  [the longest x6 10.5 us: local(): lax.ppermute(short if (k, i) == (0, CHUNKS - 1) else piece, 'dp', ring)]
    ppermute x6 -> x7, waiting for transfers between devices: 79.5 us -> 82.1 us  [the longest x6 77.7 us: local(): lax.ppermute(short if (k, i) == (0, CHUNKS - 1) else piece, 'dp', ring)]
  transfers between devices with their start and end apart: 14 -> 15, of which waited for: 5 -> 6; matrix products, arithmetic and copies ran while one was open for 0% -> 0% of each run, Pallas kernels for 10% -> 10%
where the time goes in v3:
time: 132 us; the launch traced here: 131 us
  waiting for transfers between devices  82.1 us (62%)
  Pallas kernels  18.3 us (14%)
  starting transfers between devices  15 us (11%)
  blocking collectives  14.4 us (11%)
  between operations  1.44 us (1%)
    ppermute x6, waiting for transfers between devices, local(): lax.ppermute(short if (k, i) == (0, CHUNKS - 1) else piece, 'dp', ring)  77.7 us
    all_to_all x1, blocking collectives, local(): sums = lax.all_to_all(sums, ('dp', 'mp'), 0, 0, tiled=True)  14.4 us
    ppermute x6, starting transfers between devices, local(): lax.ppermute(short if (k, i) == (0, CHUNKS - 1) else piece, 'dp', ring)  10.5 us
    pallas_call x8, Pallas kernels, place(): pl.pallas_call(functools.partial(place_pass, chips, rows, items), out_sha...  8.41 us
    pallas_call x1, Pallas kernels, local(): pl.pallas_call(first_pass, out_shape=(kept,) * 5 + (pltpu.VMEM((rows, LAN...  4.7 us
    pallas_call x1, Pallas kernels, local(): pl.pallas_call(write_pass, out_shape=(jax.ShapeDtypeStruct((rows, cols),...  4.52 us
    ppermute x1, waiting for transfers between devices, local(): pair = lax.ppermute(pair, 'dp', ring)  4.32 us
    ppermute x1, starting transfers between devices, local(): pair = lax.ppermute(pair, 'dp', ring)  2.9 us
  transfers between devices with their start and end apart: 15, of which 6 were waited for; matrix products, arithmetic and copies ran while one was open for 0% of the time, Pallas kernels for 10%

profile of v3, /device:TPU:0, one launch (start us, length us, event | category | flops | bytes accessed | tf_op | source)
XLA Modules:
  0.0 131.2 jit_solution(16845108992945132781)
XLA Ops:
  1.3 4.7 %first_pass.1 = (f32[512,1280]{1,0:T(8,128)S(1)}, f32[512,1280]{1,0:T(8,128)S(1)}, f32[512,1280]{1,0:T(8,128)S(1)}, f32[512,1280]{1,0:T(8,128)S(1)}, f32[512,128...) custom-call(s32[1]{0:T(128)S(6)} %copy.27.step_count, ...), custom_call_target="tpu_custom_call" | custom-call | tf_op jit(solution)/shard_map/first_pass/pallas_call | solution.py:222
  6.0 14.4 %all_to_all.5.sums = f32[32,2,128]{2,1,0:T(2,128)S(1)} all-to-all(f32[32,2,128]{2,1,0:T(2,128)S(1)} %get-tuple-element.19), channel_id=1, replica_groups=mesh['dp'=8,'mp'=4] {'dp','mp'}, dimensions={0} | all-to-all | bytes 65536 | tf_op jit(solution)/shard_map/all_to_all | solution.py:236
  20.7 0.7 collective-permute-start.2
  21.4 22.7 %collective-permute-done.2.refs_0_ = bf16[384,1280]{1,0:T(8,128)(2,1)S(1)} collective-permute-done((bf16[384,1280]{1,0:T(8,128)(2,1)S(1)}, bf16[384,1280]{1,0:T(8,128)(2,1)S(1)}, u32[]{:S(2)}, u32[]{:S(2)}) %collective-permute-start.2) | collective-permute-done | bytes 983072 | tf_op jit(solution)/shard_map/ppermute | solution.py:269
  44.1 1.5 %collective-permute-start.7 = (bf16[384,1280]{1,0:T(8,128)(2,1)S(1)}, bf16[384,1280]{1,0:T(8,128)(2,1)S(1)}, u32[]{:S(2)}, u32[]{:S(2)}) collective-permute-start(bf16[384,1280]{1,0:T(8,128)(2,1)S(1)} %collective-permute-done.2.refs_0_), channel_id=1, source_target_pairs={{0,16},{4,20},{16,24},{20,28},{24,8},{28,12},{8,0},{12,4},{1,17},{... | collective-permute-start | bytes 2949128 | tf_op jit(solution)/shard_map/ppermute | solution.py:269
  45.6 21.0 %collective-permute-done.7.refs_0_ = bf16[384,1280]{1,0:T(8,128)(2,1)S(1)} collective-permute-done((bf16[384,1280]{1,0:T(8,128)(2,1)S(1)}, bf16[384,1280]{1,0:T(8,128)(2,1)S(1)}, u32[]{:S(2)}, u32[]{:S(2)}) %collective-permute-start.7) | collective-permute-done | bytes 983072 | tf_op jit(solution)/shard_map/ppermute | solution.py:269
  66.6 2.4 %collective-permute-start.11 = (bf16[384,1280]{1,0:T(8,128)(2,1)S(1)}, bf16[384,1280]{1,0:T(8,128)(2,1)S(1)}, u32[]{:S(2)}, u32[]{:S(2)}) collective-permute-start(bf16[384,1280]{1,0:T(8,128)(2,1)S(1)} %collective-permute-done.7.refs_0_), channel_id=1, source_target_pairs={{0,16},{4,20},{16,24},{20,28},{24,8},{28,12},{8,0},{12,4},{1,17},{... | collective-permute-start | bytes 2949128 | tf_op jit(solution)/shard_map/ppermute | solution.py:269
  69.3 2.9 %collective-permute-start.5 = (f32[2,32,1280]{2,1,0:T(8,128)S(1)}, f32[2,32,1280]{2,1,0:T(8,128)S(1)}, u32[]{:S(2)}, u32[]{:S(2)}) collective-permute-start(f32[2,32,1280]{2,1,0:T(8,128)S(1)} %get-tuple-element.33), channel_id=1, source_target_pairs={{0,16},{4,20},{16,24},{20,28},{24,8},{28,12},{8,0},{12,4},{1,17},{... | collective-permute-start | bytes 983048 | tf_op jit(solution)/shard_map/ppermute | solution.py:235
  72.7 24.2 %collective-permute-done.4.short = bf16[96,1280]{1,0:T(8,128)(2,1)S(1)} collective-permute-done((bf16[96,1280]{1,0:T(8,128)(2,1)S(1)}, bf16[96,1280]{1,0:T(8,128)(2,1)S(1)}, u32[]{:S(2)}, u32[]{:S(2)}) %collective-permute-start.4) | collective-permute-done | bytes 245792 | tf_op jit(solution)/shard_map/ppermute | solution.py:269
  96.9 4.3 %collective-permute-done.5.pair = f32[2,32,1280]{2,1,0:T(8,128)S(1)} collective-permute-done((f32[2,32,1280]{2,1,0:T(8,128)S(1)}, f32[2,32,1280]{2,1,0:T(8,128)S(1)}, u32[]{:S(2)}, u32[]{:S(2)}) %collective-permute-start.5) | collective-permute-done | bytes 327712 | tf_op jit(solution)/shard_map/ppermute | solution.py:235
  101.4 2.7 %collective-permute-start.9 = (bf16[128,1280]{1,0:T(8,128)(2,1)S(1)}, bf16[128,1280]{1,0:T(8,128)(2,1)S(1)}, u32[]{:S(2)}, u32[]{:S(2)}) collective-permute-start(bf16[128,1280]{1,0:T(8,128)(2,1)S(1)} %merge_pass.1.refs_0_), channel_id=1, source_target_pairs={{0,16},{4,20},{16,24},{20,28},{24,8},{28,12},{8,0},{12,4},{1,17},{... | collective-permute-start | bytes 983048 | tf_op jit(solution)/shard_map/ppermute | solution.py:269
  104.6 4.8 %collective-permute-done.9.refs_0_ = bf16[128,1280]{1,0:T(8,128)(2,1)S(1)} collective-permute-done((bf16[128,1280]{1,0:T(8,128)(2,1)S(1)}, bf16[128,1280]{1,0:T(8,128)(2,1)S(1)}, u32[]{:S(2)}, u32[]{:S(2)}) %collective-permute-start.9) | collective-permute-done | bytes 327712 | tf_op jit(solution)/shard_map/ppermute | solution.py:269
  109.4 3.2 %collective-permute-start.13 = (bf16[128,1280]{1,0:T(8,128)(2,1)S(1)}, bf16[128,1280]{1,0:T(8,128)(2,1)S(1)}, u32[]{:S(2)}, u32[]{:S(2)}) collective-permute-start(bf16[128,1280]{1,0:T(8,128)(2,1)S(1)} %collective-permute-done.9.refs_0_), channel_id=1, source_target_pairs={{0,16},{4,20},{16,24},{20,28},{24,8},{28,12},{8,0},{12,4},{1,17},{... | collective-permute-start | bytes 983048 | tf_op jit(solution)/shard_map/ppermute | solution.py:269
  112.6 5.0 %collective-permute-done.13.refs_0_ = bf16[128,1280]{1,0:T(8,128)(2,1)S(1)} collective-permute-done((bf16[128,1280]{1,0:T(8,128)(2,1)S(1)}, bf16[128,1280]{1,0:T(8,128)(2,1)S(1)}, u32[]{:S(2)}, u32[]{:S(2)}) %collective-permute-start.13) | collective-permute-done | bytes 327712 | tf_op jit(solution)/shard_map/ppermute | solution.py:269
  117.6 0.5 collective-permute-start.10
  118.2 4.5 %write_pass.1 = (f32[512,1280]{1,0:T(8,128)}, f32[512,1280]{1,0:T(8,128)}, f32[512,1280]{1,0:T(8,128)}, bf16[4096,1280]{1,0:T(8,128)(2,1)}) custom-call(f32[32,2,128]{2,1,0:T(2,128)S(1)} %all_to_all.5.sums, f32[512,128]{1,0:T(8,128)S(1)} %get-tuple-element.20.member, f32[512,1280]{1,0:T(8,128)S(1)} %get-tuple-element.21.kept_master, ...), custom_call_target="tpu_custom_call" | custom-call | tf_op jit(solution)/shard_map/write_pass/pallas_call | solution.py:252
  122.7 1.1 place_pass.8.before
  123.8 1.3 %place_pass.9.before = bf16[4096,1280]{1,0:T(8,128)(2,1)} custom-call(bf16[4096,1280]{1,0:T(8,128)(2,1)} %place_pass.8.before, bf16[384,1280]{1,0:T(8,128)(2,1)S(1)} %collective-permute-done.2.refs_0_, bf16[384,1280]{1,0:T(8,128)(2,1)S(1)} %collective-permute-done.3.refs_1_), custom_call_target="tpu_custom_call", output_to_operand_aliasing={{}: (0, {})} | custom-call | tf_op jit(solution)/shard_map/place_pass/pallas_call | solution.py:200
  125.2 0.9 place_pass.10.before
  126.1 1.3 %place_pass.11.before = bf16[4096,1280]{1,0:T(8,128)(2,1)} custom-call(bf16[4096,1280]{1,0:T(8,128)(2,1)} %place_pass.10.before, bf16[384,1280]{1,0:T(8,128)(2,1)S(1)} %collective-permute-done.7.refs_0_, bf16[384,1280]{1,0:T(8,128)(2,1)S(1)} %collective-permute-done.8.refs_1_), custom_call_target="tpu_custom_call", output_to_operand_aliasing={{}: (0, {})} | custom-call | tf_op jit(solution)/shard_map/place_pass/pallas_call | solution.py:200
  127.4 0.9 place_pass.12.before
  128.3 1.3 %place_pass.13.before = bf16[4096,1280]{1,0:T(8,128)(2,1)} custom-call(bf16[4096,1280]{1,0:T(8,128)(2,1)} %place_pass.12.before, bf16[384,1280]{1,0:T(8,128)(2,1)S(1)} %collective-permute-done.11.refs_0_, bf16[384,1280]{1,0:T(8,128)(2,1)S(1)} %collective-permute-done.12.refs_1_), custom_call_target="tpu_custom_call", output_to_operand_aliasing={{}: (0, {})} | custom-call | tf_op jit(solution)/shard_map/place_pass/pallas_call | solution.py:200
  129.7 0.8 place_pass.14.before
  130.5 0.8 place_pass.15
  (20 shorter events, 1.8 us)
Async XLA Ops:
  20.7 23.4 %collective-permute-start.2 = (bf16[384,1280]{1,0:T(8,128)(2,1)S(1)}, bf16[384,1280]{1,0:T(8,128)(2,1)S(1)}, u32[]{:S(2)}, u32[]{:S(2)}) collective-permute-start(bf16[384,1280]{1,0:T(8,128)(2,1)S(1)} %round_pass.2), channel_id=1, source_target_pairs={{0,16},{4,20},{16,24},{20,28},{24,8},{28,12},{8,0},{12,4},{1,17},{... | collective-permute-start | bytes 2949128 | tf_op jit(solution)/shard_map/ppermute | solution.py:269
  44.1 22.5 %collective-permute-start.7 = (bf16[384,1280]{1,0:T(8,128)(2,1)S(1)}, bf16[384,1280]{1,0:T(8,128)(2,1)S(1)}, u32[]{:S(2)}, u32[]{:S(2)}) collective-permute-start(bf16[384,1280]{1,0:T(8,128)(2,1)S(1)} %collective-permute-done.2.refs_0_), channel_id=1, source_target_pairs={{0,16},{4,20},{16,24},{20,28},{24,8},{28,12},{8,0},{12,4},{1,17},{... | collective-permute-start | bytes 2949128 | tf_op jit(solution)/shard_map/ppermute | solution.py:269
  66.6 37.4 %collective-permute-start.11 = (bf16[384,1280]{1,0:T(8,128)(2,1)S(1)}, bf16[384,1280]{1,0:T(8,128)(2,1)S(1)}, u32[]{:S(2)}, u32[]{:S(2)}) collective-permute-start(bf16[384,1280]{1,0:T(8,128)(2,1)S(1)} %collective-permute-done.7.refs_0_), channel_id=1, source_target_pairs={{0,16},{4,20},{16,24},{20,28},{24,8},{28,12},{8,0},{12,4},{1,17},{... | collective-permute-start | bytes 2949128 | tf_op jit(solution)/shard_map/ppermute | solution.py:269
  69.2 27.7 %collective-permute-start.4 = (bf16[96,1280]{1,0:T(8,128)(2,1)S(1)}, bf16[96,1280]{1,0:T(8,128)(2,1)S(1)}, u32[]{:S(2)}, u32[]{:S(2)}) collective-permute-start(bf16[96,1280]{1,0:T(8,128)(2,1)S(1)} %get-tuple-element.32), channel_id=1, source_target_pairs={{0,16},{4,20},{16,24},{20,28},{24,8},{28,12},{8,0},{12,4},{1,17},{... | collective-permute-start | bytes 737288 | tf_op jit(solution)/shard_map/ppermute | solution.py:269
  69.3 31.9 %collective-permute-start.5 = (f32[2,32,1280]{2,1,0:T(8,128)S(1)}, f32[2,32,1280]{2,1,0:T(8,128)S(1)}, u32[]{:S(2)}, u32[]{:S(2)}) collective-permute-start(f32[2,32,1280]{2,1,0:T(8,128)S(1)} %get-tuple-element.33), channel_id=1, source_target_pairs={{0,16},{4,20},{16,24},{20,28},{24,8},{28,12},{8,0},{12,4},{1,17},{... | collective-permute-start | bytes 983048 | tf_op jit(solution)/shard_map/ppermute | solution.py:235
  72.2 31.9 %collective-permute-start.1 = (bf16[128,1280]{1,0:T(8,128)(2,1)S(1)}, bf16[128,1280]{1,0:T(8,128)(2,1)S(1)}, u32[]{:S(2)}, u32[]{:S(2)}) collective-permute-start(bf16[128,1280]{1,0:T(8,128)(2,1)S(1)} %get-tuple-element.30), channel_id=1, source_target_pairs={{0,4},{4,0},{8,12},{12,8},{16,20},{20,16},{24,28},{28,24},{1,5},{5... | collective-permute-start | bytes 983048 | tf_op jit(solution)/shard_map/ppermute | solution.py:279
  72.2 45.4 %collective-permute-start = (bf16[384,1280]{1,0:T(8,128)(2,1)S(1)}, bf16[384,1280]{1,0:T(8,128)(2,1)S(1)}, u32[]{:S(2)}, u32[]{:S(2)}) collective-permute-start(bf16[384,1280]{1,0:T(8,128)(2,1)S(1)} %round_pass.2), channel_id=1, source_target_pairs={{0,4},{4,0},{8,12},{12,8},{16,20},{20,16},{24,28},{28,24},{1,5},{5... | collective-permute-start | bytes 2949128 | tf_op jit(solution)/shard_map/ppermute | solution.py:279
  96.9 21.2 %collective-permute-start.3 = (bf16[384,1280]{1,0:T(8,128)(2,1)S(1)}, bf16[384,1280]{1,0:T(8,128)(2,1)S(1)}, u32[]{:S(2)}, u32[]{:S(2)}) collective-permute-start(bf16[384,1280]{1,0:T(8,128)(2,1)S(1)} %collective-permute-done.2.refs_0_), channel_id=1, source_target_pairs={{0,4},{4,0},{8,12},{12,8},{16,20},{20,16},{24,28},{28,24},{1,5},{5... | collective-permute-start | bytes 2949128 | tf_op jit(solution)/shard_map/ppermute | solution.py:279
  101.4 8.0 %collective-permute-start.9 = (bf16[128,1280]{1,0:T(8,128)(2,1)S(1)}, bf16[128,1280]{1,0:T(8,128)(2,1)S(1)}, u32[]{:S(2)}, u32[]{:S(2)}) collective-permute-start(bf16[128,1280]{1,0:T(8,128)(2,1)S(1)} %merge_pass.1.refs_0_), channel_id=1, source_target_pairs={{0,16},{4,20},{16,24},{20,28},{24,8},{28,12},{8,0},{12,4},{1,17},{... | collective-permute-start | bytes 983048 | tf_op jit(solution)/shard_map/ppermute | solution.py:269
  104.1 22.0 %collective-permute-start.8 = (bf16[384,1280]{1,0:T(8,128)(2,1)S(1)}, bf16[384,1280]{1,0:T(8,128)(2,1)S(1)}, u32[]{:S(2)}, u32[]{:S(2)}) collective-permute-start(bf16[384,1280]{1,0:T(8,128)(2,1)S(1)} %collective-permute-done.7.refs_0_), channel_id=1, source_target_pairs={{0,4},{4,0},{8,12},{12,8},{16,20},{20,16},{24,28},{28,24},{1,5},{5... | collective-permute-start | bytes 2949128 | tf_op jit(solution)/shard_map/ppermute | solution.py:279
  104.1 24.3 %collective-permute-start.12 = (bf16[384,1280]{1,0:T(8,128)(2,1)S(1)}, bf16[384,1280]{1,0:T(8,128)(2,1)S(1)}, u32[]{:S(2)}, u32[]{:S(2)}) collective-permute-start(bf16[384,1280]{1,0:T(8,128)(2,1)S(1)} %collective-permute-done.11.refs_0_), channel_id=1, source_target_pairs={{0,4},{4,0},{8,12},{12,8},{16,20},{20,16},{24,28},{28,24},{1,5},{5... | collective-permute-start | bytes 2949128 | tf_op jit(solution)/shard_map/ppermute | solution.py:279
  109.4 8.2 %collective-permute-start.13 = (bf16[128,1280]{1,0:T(8,128)(2,1)S(1)}, bf16[128,1280]{1,0:T(8,128)(2,1)S(1)}, u32[]{:S(2)}, u32[]{:S(2)}) collective-permute-start(bf16[128,1280]{1,0:T(8,128)(2,1)S(1)} %collective-permute-done.9.refs_0_), channel_id=1, source_target_pairs={{0,16},{4,20},{16,24},{20,28},{24,8},{28,12},{8,0},{12,4},{1,17},{... | collective-permute-start | bytes 983048 | tf_op jit(solution)/shard_map/ppermute | solution.py:269
  117.6 7.6 %collective-permute-start.6 = (bf16[128,1280]{1,0:T(8,128)(2,1)S(1)}, bf16[128,1280]{1,0:T(8,128)(2,1)S(1)}, u32[]{:S(2)}, u32[]{:S(2)}) collective-permute-start(bf16[128,1280]{1,0:T(8,128)(2,1)S(1)} %merge_pass.1.refs_0_), channel_id=1, source_target_pairs={{0,4},{4,0},{8,12},{12,8},{16,20},{20,16},{24,28},{28,24},{1,5},{5... | collective-permute-start | bytes 983048 | tf_op jit(solution)/shard_map/ppermute | solution.py:279
  117.6 9.8 %collective-permute-start.10 = (bf16[128,1280]{1,0:T(8,128)(2,1)S(1)}, bf16[128,1280]{1,0:T(8,128)(2,1)S(1)}, u32[]{:S(2)}, u32[]{:S(2)}) collective-permute-start(bf16[128,1280]{1,0:T(8,128)(2,1)S(1)} %collective-permute-done.9.refs_0_), channel_id=1, source_target_pairs={{0,4},{4,0},{8,12},{12,8},{16,20},{20,16},{24,28},{28,24},{1,5},{5... | collective-permute-start | bytes 983048 | tf_op jit(solution)/shard_map/ppermute | solution.py:279
  118.1 12.3 %collective-permute-start.14 = (bf16[128,1280]{1,0:T(8,128)(2,1)S(1)}, bf16[128,1280]{1,0:T(8,128)(2,1)S(1)}, u32[]{:S(2)}, u32[]{:S(2)}) collective-permute-start(bf16[128,1280]{1,0:T(8,128)(2,1)S(1)} %collective-permute-done.13.refs_0_), channel_id=1, source_target_pairs={{0,4},{4,0},{8,12},{12,8},{16,20},{20,16},{24,28},{28,24},{1,5},{5... | collective-permute-start | bytes 983048 | tf_op jit(solution)/shard_map/ppermute | solution.py:279

commit v4 on v3

--- a/solution.py
+++ b/solution.py
@@ -17,8 +17,8 @@
 
 LANES = 128
 TILE = 8
-PIECE = 64
-SHARES = (3, 1)
+PIECE = 128
+SHARES = (1, 2, 1)
 CHUNKS = len(SHARES)
 EARLY = 16
 MIB = 1024 * 1024
@@ -116,7 +116,7 @@
             update_rows[at] = total
             return carry
 
-        lax.fori_loop(0, size // TILE, group, 0, unroll=4)
+        lax.fori_loop(0, size // TILE, group, 0, unroll=8)
         for i in range(size // TILE):
             at = pl.ds(begin + i * TILE, TILE)
             inside = member[at]

time: 132 us -> 132 us (level)
  waiting for transfers between devices: 82.1 us -> 73.6 us
  starting transfers between devices: 15 us -> 21.5 us
  Pallas kernels: 18.3 us -> 20.4 us
    ppermute x6 -> x9, waiting for transfers between devices: 77.7 us -> 68.7 us  [local(): lax.ppermute(short if (k, i) == (0, CHUNKS - 1) else piece, 'dp', ring)]
    ppermute x6 -> x9, starting transfers between devices: 10.5 us -> 16.5 us  [local(): lax.ppermute(short if (k, i) == (0, CHUNKS - 1) else piece, 'dp', ring)]
    pallas_call x8 -> x11, Pallas kernels: 8.41 us -> 10.4 us  [place(): pl.pallas_call(functools.partial(place_pass, chips, rows, items), out_sha...]
  transfers between devices with their start and end apart: 15 -> 22, of which waited for: 6 -> 8; matrix products, arithmetic and copies ran while one was open for 0% -> 0% of each run, Pallas kernels for 10% -> 11%
where the time goes in v4:
time: 132 us
  waiting for transfers between devices  73.6 us (56%)
  starting transfers between devices  21.5 us (16%)
  Pallas kernels  20.4 us (15%)
  blocking collectives  14.4 us (11%)
  between operations  1.51 us (1%)
    ppermute x9, waiting for transfers between devices, local(): lax.ppermute(short if (k, i) == (0, CHUNKS - 1) else piece, 'dp', ring)  68.7 us
    ppermute x9, starting transfers between devices, local(): lax.ppermute(short if (k, i) == (0, CHUNKS - 1) else piece, 'dp', ring)  16.5 us
    all_to_all x1, blocking collectives, local(): sums = lax.all_to_all(sums, ('dp', 'mp'), 0, 0, tiled=True)  14.4 us
    pallas_call x11, Pallas kernels, place(): pl.pallas_call(functools.partial(place_pass, chips, rows, items), out_sha...  10.4 us
    ppermute x1, waiting for transfers between devices, local(): pair = lax.ppermute(pair, 'dp', ring)  4.9 us
    pallas_call x1, Pallas kernels, local(): pl.pallas_call(first_pass, out_shape=(kept,) * 5 + (pltpu.VMEM((rows, LAN...  4.72 us
    pallas_call x1, Pallas kernels, local(): pl.pallas_call(write_pass, out_shape=(jax.ShapeDtypeStruct((rows, cols),...  4.52 us
    ppermute x1, starting transfers between devices, local(): pair = lax.ppermute(pair, 'dp', ring)  2.89 us
  transfers between devices with their start and end apart: 22, of which 8 were waited for; matrix products, arithmetic and copies ran while one was open for 0% of the time, Pallas kernels for 11%

profile of v4, /device:TPU:0, one launch (start us, length us, event | category | flops | bytes accessed | tf_op | source)
XLA Modules:
  0.0 131.5 jit_solution(12355961728042777733)
XLA Ops:
  1.3 4.7 %first_pass.1 = (f32[512,1280]{1,0:T(8,128)S(1)}, f32[512,1280]{1,0:T(8,128)S(1)}, f32[512,1280]{1,0:T(8,128)S(1)}, f32[512,1280]{1,0:T(8,128)S(1)}, f32[512,128...) custom-call(s32[1]{0:T(128)S(6)} %copy.33.step_count, ...), custom_call_target="tpu_custom_call" | custom-call | tf_op jit(solution)/shard_map/first_pass/pallas_call | solution.py:222
  6.0 14.4 %all_to_all.5.sums = f32[32,2,128]{2,1,0:T(2,128)S(1)} all-to-all(f32[32,2,128]{2,1,0:T(2,128)S(1)} %get-tuple-element.19), channel_id=1, replica_groups=mesh['dp'=8,'mp'=4] {'dp','mp'}, dimensions={0} | all-to-all | bytes 65536 | tf_op jit(solution)/shard_map/all_to_all | solution.py:236
  21.4 15.7 %collective-permute-done.5.refs_0_ = bf16[256,1280]{1,0:T(8,128)(2,1)S(1)} collective-permute-done((bf16[256,1280]{1,0:T(8,128)(2,1)S(1)}, bf16[256,1280]{1,0:T(8,128)(2,1)S(1)}, u32[]{:S(2)}, u32[]{:S(2)}) %collective-permute-start.5) | collective-permute-done | bytes 655392 | tf_op jit(solution)/shard_map/ppermute | solution.py:269
  37.1 1.5 %collective-permute-start.12 = (bf16[256,1280]{1,0:T(8,128)(2,1)S(1)}, bf16[256,1280]{1,0:T(8,128)(2,1)S(1)}, u32[]{:S(2)}, u32[]{:S(2)}) collective-permute-start(bf16[256,1280]{1,0:T(8,128)(2,1)S(1)} %collective-permute-done.5.refs_0_), channel_id=1, source_target_pairs={{0,16},{4,20},{16,24},{20,28},{24,8},{28,12},{8,0},{12,4},{1,17},{... | collective-permute-start | bytes 1966088 | tf_op jit(solution)/shard_map/ppermute | solution.py:269
  38.8 2.9 %collective-permute-start.8 = (f32[2,32,1280]{2,1,0:T(8,128)S(1)}, f32[2,32,1280]{2,1,0:T(8,128)S(1)}, u32[]{:S(2)}, u32[]{:S(2)}) collective-permute-start(f32[2,32,1280]{2,1,0:T(8,128)S(1)} %get-tuple-element.33), channel_id=1, source_target_pairs={{0,16},{4,20},{16,24},{20,28},{24,8},{28,12},{8,0},{12,4},{1,17},{... | collective-permute-start | bytes 983048 | tf_op jit(solution)/shard_map/ppermute | solution.py:235
  42.5 17.4 %collective-permute-done.7.short = bf16[96,1280]{1,0:T(8,128)(2,1)S(1)} collective-permute-done((bf16[96,1280]{1,0:T(8,128)(2,1)S(1)}, bf16[96,1280]{1,0:T(8,128)(2,1)S(1)}, u32[]{:S(2)}, u32[]{:S(2)}) %collective-permute-start.7) | collective-permute-done | bytes 245792 | tf_op jit(solution)/shard_map/ppermute | solution.py:269
  59.9 4.9 %collective-permute-done.8.pair = f32[2,32,1280]{2,1,0:T(8,128)S(1)} collective-permute-done((f32[2,32,1280]{2,1,0:T(8,128)S(1)}, f32[2,32,1280]{2,1,0:T(8,128)S(1)}, u32[]{:S(2)}, u32[]{:S(2)}) %collective-permute-start.8) | collective-permute-done | bytes 327712 | tf_op jit(solution)/shard_map/ppermute | solution.py:235
  64.8 2.4 %collective-permute-start.3 = (bf16[128,1280]{1,0:T(8,128)(2,1)S(1)}, bf16[128,1280]{1,0:T(8,128)(2,1)S(1)}, u32[]{:S(2)}, u32[]{:S(2)}) collective-permute-start(bf16[128,1280]{1,0:T(8,128)(2,1)S(1)} %round_pass.3), channel_id=1, source_target_pairs={{0,16},{4,20},{16,24},{20,28},{24,8},{28,12},{8,0},{12,4},{1,17},{... | collective-permute-start | bytes 983048 | tf_op jit(solution)/shard_map/ppermute | solution.py:269
  67.6 2.9 %collective-permute-start.18 = (bf16[256,1280]{1,0:T(8,128)(2,1)S(1)}, bf16[256,1280]{1,0:T(8,128)(2,1)S(1)}, u32[]{:S(2)}, u32[]{:S(2)}) collective-permute-start(bf16[256,1280]{1,0:T(8,128)(2,1)S(1)} %collective-permute-done.12.refs_0_), channel_id=1, source_target_pairs={{0,16},{4,20},{16,24},{20,28},{24,8},{28,12},{8,0},{12,4},{1,17},{... | collective-permute-start | bytes 1966088 | tf_op jit(solution)/shard_map/ppermute | solution.py:269
  70.5 5.1 %collective-permute-done.3.refs_0_ = bf16[128,1280]{1,0:T(8,128)(2,1)S(1)} collective-permute-done((bf16[128,1280]{1,0:T(8,128)(2,1)S(1)}, bf16[128,1280]{1,0:T(8,128)(2,1)S(1)}, u32[]{:S(2)}, u32[]{:S(2)}) %collective-permute-start.3) | collective-permute-done | bytes 327712 | tf_op jit(solution)/shard_map/ppermute | solution.py:269
  75.6 3.1 %collective-permute-start.10 = (bf16[128,1280]{1,0:T(8,128)(2,1)S(1)}, bf16[128,1280]{1,0:T(8,128)(2,1)S(1)}, u32[]{:S(2)}, u32[]{:S(2)}) collective-permute-start(bf16[128,1280]{1,0:T(8,128)(2,1)S(1)} %collective-permute-done.3.refs_0_), channel_id=1, source_target_pairs={{0,16},{4,20},{16,24},{20,28},{24,8},{28,12},{8,0},{12,4},{1,17},{... | collective-permute-start | bytes 983048 | tf_op jit(solution)/shard_map/ppermute | solution.py:269
  78.7 3.9 %collective-permute-done.14.refs_0_ = bf16[128,1280]{1,0:T(8,128)(2,1)S(1)} collective-permute-done((bf16[128,1280]{1,0:T(8,128)(2,1)S(1)}, bf16[128,1280]{1,0:T(8,128)(2,1)S(1)}, u32[]{:S(2)}, u32[]{:S(2)}) %collective-permute-start.14) | collective-permute-done | bytes 327712 | tf_op jit(solution)/shard_map/ppermute | solution.py:269
  82.6 3.1 %collective-permute-start.20 = (bf16[128,1280]{1,0:T(8,128)(2,1)S(1)}, bf16[128,1280]{1,0:T(8,128)(2,1)S(1)}, u32[]{:S(2)}, u32[]{:S(2)}) collective-permute-start(bf16[128,1280]{1,0:T(8,128)(2,1)S(1)} %collective-permute-done.14.refs_0_), channel_id=1, source_target_pairs={{0,16},{4,20},{16,24},{20,28},{24,8},{28,12},{8,0},{12,4},{1,17},{... | collective-permute-start | bytes 983048 | tf_op jit(solution)/shard_map/ppermute | solution.py:269
  86.3 17.4 %collective-permute-done.10.refs_0_ = bf16[128,1280]{1,0:T(8,128)(2,1)S(1)} collective-permute-done((bf16[128,1280]{1,0:T(8,128)(2,1)S(1)}, bf16[128,1280]{1,0:T(8,128)(2,1)S(1)}, u32[]{:S(2)}, u32[]{:S(2)}) %collective-permute-start.10) | collective-permute-done | bytes 327712 | tf_op jit(solution)/shard_map/ppermute | solution.py:269
  103.7 4.5 %collective-permute-done.20.refs_0_ = bf16[128,1280]{1,0:T(8,128)(2,1)S(1)} collective-permute-done((bf16[128,1280]{1,0:T(8,128)(2,1)S(1)}, bf16[128,1280]{1,0:T(8,128)(2,1)S(1)}, u32[]{:S(2)}, u32[]{:S(2)}) %collective-permute-start.20) | collective-permute-done | bytes 327712 | tf_op jit(solution)/shard_map/ppermute | solution.py:269
  108.2 2.6 %collective-permute-start.16 = (bf16[128,1280]{1,0:T(8,128)(2,1)S(1)}, bf16[128,1280]{1,0:T(8,128)(2,1)S(1)}, u32[]{:S(2)}, u32[]{:S(2)}) collective-permute-start(bf16[128,1280]{1,0:T(8,128)(2,1)S(1)} %collective-permute-done.10.refs_0_), channel_id=1, source_target_pairs={{0,16},{4,20},{16,24},{20,28},{24,8},{28,12},{8,0},{12,4},{1,17},{... | collective-permute-start | bytes 983048 | tf_op jit(solution)/shard_map/ppermute | solution.py:269
  111.4 4.5 %collective-permute-done.16.refs_0_ = bf16[128,1280]{1,0:T(8,128)(2,1)S(1)} collective-permute-done((bf16[128,1280]{1,0:T(8,128)(2,1)S(1)}, bf16[128,1280]{1,0:T(8,128)(2,1)S(1)}, u32[]{:S(2)}, u32[]{:S(2)}) %collective-permute-start.16) | collective-permute-done | bytes 327712 | tf_op jit(solution)/shard_map/ppermute | solution.py:269
  116.4 4.5 %write_pass.1 = (f32[512,1280]{1,0:T(8,128)}, f32[512,1280]{1,0:T(8,128)}, f32[512,1280]{1,0:T(8,128)}, bf16[4096,1280]{1,0:T(8,128)(2,1)}) custom-call(f32[32,2,128]{2,1,0:T(2,128)S(1)} %all_to_all.5.sums, f32[512,128]{1,0:T(8,128)S(1)} %get-tuple-element.20.member, f32[512,1280]{1,0:T(8,128)S(1)} %get-tuple-element.21.kept_master, ...), custom_call_target="tpu_custom_call" | custom-call | tf_op jit(solution)/shard_map/write_pass/pallas_call | solution.py:252
  120.9 1.1 place_pass.11.before
  123.0 1.1 place_pass.13.before
  124.1 0.9 place_pass.14.before
  125.9 1.1 place_pass.16.before
  127.0 0.9 place_pass.17.before
  128.8 1.1 place_pass.19.before
  (38 shorter events, 8.0 us)
Async XLA Ops:
  20.7 16.4 %collective-permute-start.5 = (bf16[256,1280]{1,0:T(8,128)(2,1)S(1)}, bf16[256,1280]{1,0:T(8,128)(2,1)S(1)}, u32[]{:S(2)}, u32[]{:S(2)}) collective-permute-start(bf16[256,1280]{1,0:T(8,128)(2,1)S(1)} %round_pass.4), channel_id=1, source_target_pairs={{0,16},{4,20},{16,24},{20,28},{24,8},{28,12},{8,0},{12,4},{1,17},{... | collective-permute-start | bytes 1966088 | tf_op jit(solution)/shard_map/ppermute | solution.py:269
  37.1 30.5 %collective-permute-start.12 = (bf16[256,1280]{1,0:T(8,128)(2,1)S(1)}, bf16[256,1280]{1,0:T(8,128)(2,1)S(1)}, u32[]{:S(2)}, u32[]{:S(2)}) collective-permute-start(bf16[256,1280]{1,0:T(8,128)(2,1)S(1)} %collective-permute-done.5.refs_0_), channel_id=1, source_target_pairs={{0,16},{4,20},{16,24},{20,28},{24,8},{28,12},{8,0},{12,4},{1,17},{... | collective-permute-start | bytes 1966088 | tf_op jit(solution)/shard_map/ppermute | solution.py:269
  38.8 21.2 %collective-permute-start.7 = (bf16[96,1280]{1,0:T(8,128)(2,1)S(1)}, bf16[96,1280]{1,0:T(8,128)(2,1)S(1)}, u32[]{:S(2)}, u32[]{:S(2)}) collective-permute-start(bf16[96,1280]{1,0:T(8,128)(2,1)S(1)} %get-tuple-element.32), channel_id=1, source_target_pairs={{0,16},{4,20},{16,24},{20,28},{24,8},{28,12},{8,0},{12,4},{1,17},{... | collective-permute-start | bytes 737288 | tf_op jit(solution)/shard_map/ppermute | solution.py:269
  38.8 26.0 %collective-permute-start.8 = (f32[2,32,1280]{2,1,0:T(8,128)S(1)}, f32[2,32,1280]{2,1,0:T(8,128)S(1)}, u32[]{:S(2)}, u32[]{:S(2)}) collective-permute-start(f32[2,32,1280]{2,1,0:T(8,128)S(1)} %get-tuple-element.33), channel_id=1, source_target_pairs={{0,16},{4,20},{16,24},{20,28},{24,8},{28,12},{8,0},{12,4},{1,17},{... | collective-permute-start | bytes 983048 | tf_op jit(solution)/shard_map/ppermute | solution.py:235
  41.7 25.7 %collective-permute-start.2 = (bf16[128,1280]{1,0:T(8,128)(2,1)S(1)}, bf16[128,1280]{1,0:T(8,128)(2,1)S(1)}, u32[]{:S(2)}, u32[]{:S(2)}) collective-permute-start(bf16[128,1280]{1,0:T(8,128)(2,1)S(1)} %get-tuple-element.30), channel_id=1, source_target_pairs={{0,4},{4,0},{8,12},{12,8},{16,20},{20,16},{24,28},{28,24},{1,5},{5... | collective-permute-start | bytes 983048 | tf_op jit(solution)/shard_map/ppermute | solution.py:279
  41.9 25.6 %collective-permute-start = (bf16[128,1280]{1,0:T(8,128)(2,1)S(1)}, bf16[128,1280]{1,0:T(8,128)(2,1)S(1)}, u32[]{:S(2)}, u32[]{:S(2)}) collective-permute-start(bf16[128,1280]{1,0:T(8,128)(2,1)S(1)} %round_pass.3), channel_id=1, source_target_pairs={{0,4},{4,0},{8,12},{12,8},{16,20},{20,16},{24,28},{28,24},{1,5},{5... | collective-permute-start | bytes 983048 | tf_op jit(solution)/shard_map/ppermute | solution.py:279
  59.9 25.8 %collective-permute-start.1 = (bf16[256,1280]{1,0:T(8,128)(2,1)S(1)}, bf16[256,1280]{1,0:T(8,128)(2,1)S(1)}, u32[]{:S(2)}, u32[]{:S(2)}) collective-permute-start(bf16[256,1280]{1,0:T(8,128)(2,1)S(1)} %round_pass.4), channel_id=1, source_target_pairs={{0,4},{4,0},{8,12},{12,8},{16,20},{20,16},{24,28},{28,24},{1,5},{5... | collective-permute-start | bytes 1966088 | tf_op jit(solution)/shard_map/ppermute | solution.py:279
  64.8 10.8 %collective-permute-start.3 = (bf16[128,1280]{1,0:T(8,128)(2,1)S(1)}, bf16[128,1280]{1,0:T(8,128)(2,1)S(1)}, u32[]{:S(2)}, u32[]{:S(2)}) collective-permute-start(bf16[128,1280]{1,0:T(8,128)(2,1)S(1)} %round_pass.3), channel_id=1, source_target_pairs={{0,16},{4,20},{16,24},{20,28},{24,8},{28,12},{8,0},{12,4},{1,17},{... | collective-permute-start | bytes 983048 | tf_op jit(solution)/shard_map/ppermute | solution.py:269
  67.4 8.2 %collective-permute-start.9 = (bf16[128,1280]{1,0:T(8,128)(2,1)S(1)}, bf16[128,1280]{1,0:T(8,128)(2,1)S(1)}, u32[]{:S(2)}, u32[]{:S(2)}) collective-permute-start(bf16[128,1280]{1,0:T(8,128)(2,1)S(1)} %merge_pass.1.refs_0_), channel_id=1, source_target_pairs={{0,4},{4,0},{8,12},{12,8},{16,20},{20,16},{24,28},{28,24},{1,5},{5... | collective-permute-start | bytes 983048 | tf_op jit(solution)/shard_map/ppermute | solution.py:279
  67.5 15.1 %collective-permute-start.14 = (bf16[128,1280]{1,0:T(8,128)(2,1)S(1)}, bf16[128,1280]{1,0:T(8,128)(2,1)S(1)}, u32[]{:S(2)}, u32[]{:S(2)}) collective-permute-start(bf16[128,1280]{1,0:T(8,128)(2,1)S(1)} %merge_pass.1.refs_0_), channel_id=1, source_target_pairs={{0,16},{4,20},{16,24},{20,28},{24,8},{28,12},{8,0},{12,4},{1,17},{... | collective-permute-start | bytes 983048 | tf_op jit(solution)/shard_map/ppermute | solution.py:269
  67.6 43.3 %collective-permute-start.18 = (bf16[256,1280]{1,0:T(8,128)(2,1)S(1)}, bf16[256,1280]{1,0:T(8,128)(2,1)S(1)}, u32[]{:S(2)}, u32[]{:S(2)}) collective-permute-start(bf16[256,1280]{1,0:T(8,128)(2,1)S(1)} %collective-permute-done.12.refs_0_), channel_id=1, source_target_pairs={{0,16},{4,20},{16,24},{20,28},{24,8},{28,12},{8,0},{12,4},{1,17},{... | collective-permute-start | bytes 1966088 | tf_op jit(solution)/shard_map/ppermute | solution.py:269
  75.6 10.2 %collective-permute-start.4 = (bf16[128,1280]{1,0:T(8,128)(2,1)S(1)}, bf16[128,1280]{1,0:T(8,128)(2,1)S(1)}, u32[]{:S(2)}, u32[]{:S(2)}) collective-permute-start(bf16[128,1280]{1,0:T(8,128)(2,1)S(1)} %collective-permute-done.3.refs_0_), channel_id=1, source_target_pairs={{0,4},{4,0},{8,12},{12,8},{16,20},{20,16},{24,28},{28,24},{1,5},{5... | collective-permute-start | bytes 983048 | tf_op jit(solution)/shard_map/ppermute | solution.py:279
  75.6 28.1 %collective-permute-start.10 = (bf16[128,1280]{1,0:T(8,128)(2,1)S(1)}, bf16[128,1280]{1,0:T(8,128)(2,1)S(1)}, u32[]{:S(2)}, u32[]{:S(2)}) collective-permute-start(bf16[128,1280]{1,0:T(8,128)(2,1)S(1)} %collective-permute-done.3.refs_0_), channel_id=1, source_target_pairs={{0,16},{4,20},{16,24},{20,28},{24,8},{28,12},{8,0},{12,4},{1,17},{... | collective-permute-start | bytes 983048 | tf_op jit(solution)/shard_map/ppermute | solution.py:269
  82.6 25.6 %collective-permute-start.20 = (bf16[128,1280]{1,0:T(8,128)(2,1)S(1)}, bf16[128,1280]{1,0:T(8,128)(2,1)S(1)}, u32[]{:S(2)}, u32[]{:S(2)}) collective-permute-start(bf16[128,1280]{1,0:T(8,128)(2,1)S(1)} %collective-permute-done.14.refs_0_), channel_id=1, source_target_pairs={{0,16},{4,20},{16,24},{20,28},{24,8},{28,12},{8,0},{12,4},{1,17},{... | collective-permute-start | bytes 983048 | tf_op jit(solution)/shard_map/ppermute | solution.py:269
  85.7 30.2 %collective-permute-start.6 = (bf16[256,1280]{1,0:T(8,128)(2,1)S(1)}, bf16[256,1280]{1,0:T(8,128)(2,1)S(1)}, u32[]{:S(2)}, u32[]{:S(2)}) collective-permute-start(bf16[256,1280]{1,0:T(8,128)(2,1)S(1)} %collective-permute-done.5.refs_0_), channel_id=1, source_target_pairs={{0,4},{4,0},{8,12},{12,8},{16,20},{20,16},{24,28},{28,24},{1,5},{5... | collective-permute-start | bytes 1966088 | tf_op jit(solution)/shard_map/ppermute | solution.py:279
  85.8 40.1 %collective-permute-start.13 = (bf16[256,1280]{1,0:T(8,128)(2,1)S(1)}, bf16[256,1280]{1,0:T(8,128)(2,1)S(1)}, u32[]{:S(2)}, u32[]{:S(2)}) collective-permute-start(bf16[256,1280]{1,0:T(8,128)(2,1)S(1)} %collective-permute-done.12.refs_0_), channel_id=1, source_target_pairs={{0,4},{4,0},{8,12},{12,8},{16,20},{20,16},{24,28},{28,24},{1,5},{5... | collective-permute-start | bytes 1966088 | tf_op jit(solution)/shard_map/ppermute | solution.py:279
  103.7 7.2 %collective-permute-start.11 = (bf16[128,1280]{1,0:T(8,128)(2,1)S(1)}, bf16[128,1280]{1,0:T(8,128)(2,1)S(1)}, u32[]{:S(2)}, u32[]{:S(2)}) collective-permute-start(bf16[128,1280]{1,0:T(8,128)(2,1)S(1)} %collective-permute-done.10.refs_0_), channel_id=1, source_target_pairs={{0,4},{4,0},{8,12},{12,8},{16,20},{20,16},{24,28},{28,24},{1,5},{5... | collective-permute-start | bytes 983048 | tf_op jit(solution)/shard_map/ppermute | solution.py:279
  108.2 7.7 %collective-permute-start.16 = (bf16[128,1280]{1,0:T(8,128)(2,1)S(1)}, bf16[128,1280]{1,0:T(8,128)(2,1)S(1)}, u32[]{:S(2)}, u32[]{:S(2)}) collective-permute-start(bf16[128,1280]{1,0:T(8,128)(2,1)S(1)} %collective-permute-done.10.refs_0_), channel_id=1, source_target_pairs={{0,16},{4,20},{16,24},{20,28},{24,8},{28,12},{8,0},{12,4},{1,17},{... | collective-permute-start | bytes 983048 | tf_op jit(solution)/shard_map/ppermute | solution.py:269
  110.8 18.0 %collective-permute-start.19 = (bf16[256,1280]{1,0:T(8,128)(2,1)S(1)}, bf16[256,1280]{1,0:T(8,128)(2,1)S(1)}, u32[]{:S(2)}, u32[]{:S(2)}) collective-permute-start(bf16[256,1280]{1,0:T(8,128)(2,1)S(1)} %collective-permute-done.18.refs_0_), channel_id=1, source_target_pairs={{0,4},{4,0},{8,12},{12,8},{16,20},{20,16},{24,28},{28,24},{1,5},{5... | collective-permute-start | bytes 1966088 | tf_op jit(solution)/shard_map/ppermute | solution.py:279
  110.9 16.1 %collective-permute-start.15 = (bf16[128,1280]{1,0:T(8,128)(2,1)S(1)}, bf16[128,1280]{1,0:T(8,128)(2,1)S(1)}, u32[]{:S(2)}, u32[]{:S(2)}) collective-permute-start(bf16[128,1280]{1,0:T(8,128)(2,1)S(1)} %collective-permute-done.14.refs_0_), channel_id=1, source_target_pairs={{0,4},{4,0},{8,12},{12,8},{16,20},{20,16},{24,28},{28,24},{1,5},{5... | collective-permute-start | bytes 983048 | tf_op jit(solution)/shard_map/ppermute | solution.py:279
  115.9 12.0 %collective-permute-start.17 = (bf16[128,1280]{1,0:T(8,128)(2,1)S(1)}, bf16[128,1280]{1,0:T(8,128)(2,1)S(1)}, u32[]{:S(2)}, u32[]{:S(2)}) collective-permute-start(bf16[128,1280]{1,0:T(8,128)(2,1)S(1)} %collective-permute-done.16.refs_0_), channel_id=1, source_target_pairs={{0,4},{4,0},{8,12},{12,8},{16,20},{20,16},{24,28},{28,24},{1,5},{5... | collective-permute-start | bytes 983048 | tf_op jit(solution)/shard_map/ppermute | solution.py:279
  115.9 14.8 %collective-permute-start.21 = (bf16[128,1280]{1,0:T(8,128)(2,1)S(1)}, bf16[128,1280]{1,0:T(8,128)(2,1)S(1)}, u32[]{:S(2)}, u32[]{:S(2)}) collective-permute-start(bf16[128,1280]{1,0:T(8,128)(2,1)S(1)} %collective-permute-done.20.refs_0_), channel_id=1, source_target_pairs={{0,4},{4,0},{8,12},{12,8},{16,20},{20,16},{24,28},{28,24},{1,5},{5... | collective-permute-start | bytes 983048 | tf_op jit(solution)/shard_map/ppermute | solution.py:279
